TPU v7x, 32 devices: a whole 2x2x4 slice. The times are simulated.
32 devices in a mesh: rep: 2 (over x), gx: 16 (over z, y, core).
Axes of the slice: x: 2, y: 2, z: 4, core: 2. Of those that a mesh axis runs over, the one named last changes fastest.
Arguments:
- positions: float32 [3, 131072], P(None, ('rep', 'gx')), parts along dimension 1, may hold values from 0 to 128, as said below
- polar: float32 [131072], P(('rep', 'gx')), parts along dimension 0, may hold values from 0.25 to 1
- field_ext: float32 [3, 131072], P(None, ('rep', 'gx')), parts along dimension 1, may hold values from -10 to 10
- tile_atom: int32 [131072], P(('rep', 'gx')), parts along dimension 0, may hold values from 0 to 4095, as said below
- tile_list: int32 [1024, 3], P(('rep', 'gx')), parts along dimension 0, may hold values from 0 to 63, as said below
- image_shift: int32 [2, 1024, 3], P(None, ('rep', 'gx')), parts along dimension 1, may hold values from 0 to 1, as said below
Outputs:
- dipoles: float32 [3, 131072], P(None, ('rep', 'gx')), parts along dimension 1
- residual: float32 [3, 131072], P(None, ('rep', 'gx')), parts along dimension 1
There are 2 independent parts, one for each index of `rep`. A program takes and returns all parts, laid end to end along the dimension named above; each array names one. Nothing has to cross between parts.
Inputs may be any that keep to these rules, and one draw needn't show every extreme that they name: `positions`: coordinates lie in a box of 64 by 128 by 64; the atoms of slab s have first coordinate between 4 s and 4 s + 4; no two atoms, and no atom and a periodic image of another, are closer than 1.4. `tile_atom`: for each slab, a permutation of 0 to 4095. `tile_list`: entry 0 of a tile is the tile's own index within its slab. Entry n of a tile of slab s names tile n of slab s if n < 32, else tile n - 32 of slab s + 1 (slab 0 after the last). `image_shift`: offsets along the second and third coordinates in box lengths, one pair for each entry of tile_list; zero for entry 0.
All inputs are finite; a program needn't handle non-finite values.
Results may differ from a plain program's by a relative error of at most 0.0003.
Values sent between devices are 32-bit elements; how exact they have to be, the bound alone decides.
A program may use at most 64 MiB of HBM per device.

v0:
```python
import functools

import jax
import jax.numpy as jnp
from jax import lax
from jax.experimental import pallas as pl
from jax.experimental.pallas import tpu as pltpu
from jax.sharding import PartitionSpec as P

ITERS = 4
MESH = pl.DeviceIdType.MESH
thole_factor = 0.39
ROWS = 16
F32 = jnp.float32
BF16 = jnp.bfloat16


def split_two(value):
    high = value.astype(BF16)
    return high, (value - high.astype(F32)).astype(BF16)


def split_three(value):
    high = value.astype(BF16)
    rest = value - high.astype(F32)
    middle = rest.astype(BF16)
    return high, middle, (rest - middle.astype(F32)).astype(BF16)


def gather_tile(row, source, tiles):
    width = 128
    inner = jnp.broadcast_to(row & (width - 1), (8, width))
    outer = jnp.broadcast_to(row >> 7, (8, width))
    value = jnp.zeros((8, width), F32)
    for tile in range(tiles):
        picked = jnp.take_along_axis(
            source[pl.ds(tile * 8, 8), :], inner, axis=1, mode="promise_in_bounds"
        )
        value = jnp.where(outer == tile, picked, value)
    return value


def tiling_kernel(
    tiles,
    links,
    list_ref,
    shift_ref,
    place_ref,
    polar_ref,
    field_ref,
    atom_ref,
    out_ref,
    inverse,
    hits,
    image,
    feat,
):
    width = 128
    near = links - 1
    for tile in range(tiles):
        lanes = pl.ds(tile * width, width)
        feat[tile * 8 : tile * 8 + 3, :] = place_ref[:, lanes]
        feat[tile * 8 + 3 : tile * 8 + 6, :] = field_ref[:, lanes]
        feat[tile * 8 + 6 : tile * 8 + 7, :] = polar_ref[:, lanes]
        feat[tile * 8 + 7 : tile * 8 + 8, :] = jnp.ones((1, width), F32)
    sub_ids = lax.broadcasted_iota(jnp.int32, (8, width), 0)

    def fill(tile, carry):
        value = gather_tile(atom_ref[pl.ds(tile, 1), :], feat, tiles)
        root = lax.rsqrt(value)
        value = jnp.where(sub_ids == 7, pltpu.roll(root, 1, 0), value)
        out_ref[pl.ds(pl.multiple_of(tile * 8, 8), 8), :] = value
        return carry

    lax.fori_loop(0, tiles, fill, 0, unroll=4)

    lane_ids = lax.broadcasted_iota(jnp.int32, (width, width), 0)
    tile_ids = lax.broadcasted_iota(jnp.int32, (tiles, width), 0)
    lane_row = lax.broadcasted_iota(jnp.int32, (tiles, width), 1).astype(F32)

    def invert(tile, total):
        row = atom_ref[pl.ds(tile, 1), :]
        outer = tile_ids == (row >> 7)
        number = jnp.full((tiles, width), tile, jnp.int32).astype(F32)
        left = jnp.concatenate(
            [jnp.where(outer, number, 0.0), jnp.where(outer, lane_row, 0.0)], axis=0
        ).astype(BF16)
        right = jnp.where(lane_ids == (row & (width - 1)), 1.0, 0.0).astype(BF16)
        return total + lax.dot_general(
            left, right, (((1,), (1,)), ((), ())), preferred_element_type=F32
        )

    found = lax.fori_loop(
        0, tiles, invert, jnp.zeros((2 * tiles, width), F32), unroll=4
    )
    inverse[...] = (found[:tiles] * float(width) + found[tiles:]).astype(jnp.int32)

    lane_one = lax.broadcasted_iota(jnp.int32, (1, width), 1)

    def name(tile, carry):
        for entry in range(near):
            slot = entry * tiles + tile
            named = list_ref[tile * links + entry + 1]
            hit = jnp.where((lane_one == named) | (lane_one == named + 2 * tiles), 1.0, 0.0)
            hits[pl.ds(slot, 1), :] = hit
            hits[pl.ds(near * tiles + slot, 1), :] = hit
            ones = jnp.ones((1, width), F32)
            crossing = jnp.where(named >= tiles, 1.0, 0.0)
            step_y = shift_ref[tile * links + entry + 1].astype(F32)
            step_z = shift_ref[(tiles + tile) * links + entry + 1].astype(F32)
            image[0, pl.ds(slot, 1), :] = ones * crossing
            image[1, pl.ds(slot, 1), :] = ones * step_y
            image[2, pl.ds(slot, 1), :] = ones * step_z
        return carry

    lax.fori_loop(0, tiles, name, 0, unroll=4)


def untiling_kernel(tiles, tiled_ref, inverse, dip_ref, res_ref):
    width = 128

    def give(tile, carry):
        value = gather_tile(inverse[pl.ds(tile, 1), :], tiled_ref, tiles)
        lanes = pl.ds(pl.multiple_of(tile * width, width), width)
        dip_ref[:, lanes] = value[0:3]
        res_ref[:, lanes] = value[3:6]
        return carry

    lax.fori_loop(0, tiles, give, 0, unroll=4)


def kernel(
    count,
    tiles,
    links,
    tiled_ref,
    hits_ref,
    image_ref,
    out_ref,
    window,
    pair_own,
    pair_back,
    pair_left,
    three_t,
    five_t,
    there,
    local,
    local_far,
    shift_left,
    shift_right,
    moments,
    minus,
    results,
    sent_w,
    ahead_w,
    sent_f,
    back_f,
    dots,
    pack_sem,
    w_sem,
    f_sem,
    dot_sem,
):
    width = 128
    near = links - 1
    me = lax.axis_index("gx")
    after = lax.rem(me + 1, count)
    before = lax.rem(me + count - 1, count)

    barrier = pltpu.get_barrier_semaphore()

    def greet(step, carry):
        pl.semaphore_signal(
            barrier, inc=1, device_id={"gx": lax.rem(me + step, count)}, device_id_type=MESH
        )
        return carry

    lax.fori_loop(1, count, greet, 0)

    sub_ids = lax.broadcasted_iota(jnp.int32, (8, width), 0)

    window[0 : tiles * 8, :] = tiled_ref[...]
    pl.semaphore_wait(barrier, count - 1)
    pack_copy = pltpu.make_async_remote_copy(
        src_ref=tiled_ref,
        dst_ref=window.at[pl.ds(tiles * 8, tiles * 8)],
        send_sem=pack_sem.at[0],
        recv_sem=pack_sem.at[1],
        device_id={"gx": before},
        device_id_type=MESH,
    )
    pack_copy.start()

    row_ids = lax.broadcasted_iota(jnp.int32, (16, width), 0)
    column_ids = lax.broadcasted_iota(jnp.int32, (16, width), 1)

    def pair_rows(columns, other, first, same):
        rows = slice(first, first + 16)
        off_x = other[0:1, :] - columns[rows, 0:1]
        off_y = other[1:2, :] - columns[rows, 1:2]
        off_z = other[2:3, :] - columns[rows, 2:3]
        dist_sq = off_x * off_x + off_y * off_y + off_z * off_z
        if same:
            mask = row_ids + first == column_ids
            dist_sq = jnp.where(mask, 1.0, dist_sq)
        inv = lax.rsqrt(dist_sq)
        inv_sq = inv * inv
        damp = dist_sq * dist_sq * inv * (columns[rows, 7:8] * (thole_factor * other[7:8, :]))
        decay = jnp.exp(-damp)
        inv_cube = inv * inv_sq
        if same:
            inv_cube = jnp.where(mask, 0.0, inv_cube)
        less = 1.0 - decay
        three = less * inv_cube
        five = 3.0 * (less - damp * decay) * (inv_cube * inv_sq)
        return three, five

    def store_pair(target, index, first, three, five):
        rows = slice(first, first + 16)
        more = slice(width + first, width + first + 16)
        high, low = split_two(five)
        target[index, rows, 0:width] = high
        target[index, rows, width : 2 * width] = low
        high, low = split_two(three)
        target[index, more, 0:width] = high
        target[index, more, width : 2 * width] = low

    def own_pairs(tile, carry):
        here = window[pl.ds(pl.multiple_of(tile * 8, 8), 8), :]
        columns = here.T
        for first in range(0, width, 16):
            three, five = pair_rows(columns, here, first, True)
            store_pair(pair_own, tile, first, three, five)
        return carry

    lax.fori_loop(0, tiles, own_pairs, 0)

    pack_copy.wait_recv()

    slots = near * tiles
    hit_own = hits_ref[0:slots, :].astype(BF16)
    hit_rows = hits_ref[...].T[0 : 2 * tiles].astype(BF16)

    def picked(matrix, values):
        high, middle, low = split_three(jnp.concatenate(values, axis=1))
        found = jnp.dot(
            matrix, jnp.concatenate([high, middle], axis=0), preferred_element_type=F32
        ) + jnp.dot(
            matrix,
            jnp.concatenate([low, jnp.zeros_like(low)], axis=0),
            preferred_element_type=F32,
        )
        return [found[:, part * width : (part + 1) * width] for part in range(len(values))]

    def middle_of(value):
        return jnp.floor(jnp.mean(value, axis=1, keepdims=True) + 0.5)

    both = [window[pl.ds(row, 2 * tiles, stride=8), :] for row in (0, 1, 2, 7)]
    named = picked(hit_own, both)
    there[pl.ds(7, slots, stride=8), :] = named[3]
    lengths = (jnp.where(me == count - 1, 4.0 * count, 0.0), 128.0, 2.0 * tiles)
    for axis in range(3):
        here = both[axis][0:tiles]
        here_middle = middle_of(here)
        local[axis] = here - here_middle
        far_middle = middle_of(named[axis])
        local_far[axis] = named[axis] - far_middle
        vector = image_ref[axis] * lengths[axis]
        moved = named[axis] + vector
        there[pl.ds(axis, slots, stride=8), :] = moved
        for entry in range(near):
            part = slice(entry * tiles, (entry + 1) * tiles)
            shift_left[axis, part, :] = here - (far_middle[part] + vector[part])
            shift_right[axis, part, :] = moved[part] - here_middle

    def far_pairs(tile, carry):
        here_rows = pl.ds(pl.multiple_of(tile * 8, 8), 8)
        here = window[here_rows, :]
        columns = here.T
        for entry in range(near):
            slot = entry * tiles + tile
            other = there[pl.ds(pl.multiple_of(slot * 8, 8), 8), :]
            for first in range(0, width, 16):
                three, five = pair_rows(columns, other, first, False)
                store_pair(pair_back, slot, first, three, five)
                three_t[entry, first : first + 16, :] = three
                five_t[entry, first : first + 16, :] = five
            three = three_t[entry].T
            five = five_t[entry].T
            for first in range(0, width, 16):
                store_pair(
                    pair_left, slot, first, three[first : first + 16], five[first : first + 16]
                )
        return carry

    lax.fori_loop(0, tiles, far_pairs, 0)
    minus[...] = jnp.zeros_like(minus)

    def build(vec, base_ref, size):
        base = [base_ref[axis] for axis in range(3)]
        along = base[0] * vec[0] + base[1] * vec[1] + base[2] * vec[2]

        def put(ref, row, value):
            ref[pl.ds(row, size, stride=ROWS), :] = value

        for axis in range(3):
            put(moments, axis, base[axis] * along)
            put(minus, axis, -vec[axis])
            for other in range(3):
                put(moments, 4 + 4 * axis + other, base[other] * vec[axis])
            put(moments, 7 + 4 * axis, vec[axis])
        put(moments, 3, along)

    def block_of(tile):
        rows = pl.ds(pl.multiple_of(tile * ROWS, ROWS), ROWS)
        return jnp.concatenate(
            [
                jnp.concatenate(split_three(moments[rows, :]), axis=0),
                jnp.concatenate(split_three(minus[rows, :]), axis=0),
            ],
            axis=1,
        )

    def product(block, weights, slot):
        out = jnp.dot(block, weights, preferred_element_type=F32)
        out = out[:, :width] + out[:, width:]
        results[pl.ds(pl.multiple_of(slot * ROWS, ROWS), ROWS), :] = (
            out[0:ROWS] + out[ROWS : 2 * ROWS]
        ) + out[2 * ROWS : 3 * ROWS]

    def combined(kind, shifts):
        def get(row):
            return results[pl.ds(kind * tiles * ROWS + row, tiles, stride=ROWS), :]

        parts = []
        for row in range(4):
            total = get(row)
            for axis in range(3):
                total = total - shifts[axis] * get(4 + 4 * axis + row)
            parts.append(total)
        return [parts[axis] - shifts[axis] * parts[3] for axis in range(3)]

    def shifts_of(ref, entry):
        return [ref[axis, entry * tiles : (entry + 1) * tiles, :] for axis in range(3)]

    alpha_inv = 1.0 / window[pl.ds(6, tiles, stride=8), :]

    def copy_w(turn):
        return pltpu.make_async_remote_copy(
            src_ref=sent_w.at[turn],
            dst_ref=ahead_w.at[turn],
            send_sem=w_sem.at[0, turn],
            recv_sem=w_sem.at[1, turn],
            device_id={"gx": before},
            device_id_type=MESH,
        )

    def copy_f(turn):
        return pltpu.make_async_remote_copy(
            src_ref=sent_f.at[turn],
            dst_ref=back_f.at[turn],
            send_sem=f_sem.at[0, turn],
            recv_sem=f_sem.at[1, turn],
            device_id={"gx": after},
            device_id_type=MESH,
        )

    def back_step(group, carry):
        for offset in range(4):
            tile = group * 4 + offset
            block = block_of(tile)
            product(block, pair_own[tile], tile)
            for entry in range(near):
                slot = entry * tiles + tile
                product(block, pair_back[slot], tiles + slot)
        return carry

    def left_step(group, carry):
        for offset in range(4):
            tile = group * 4 + offset
            for entry in range(near):
                slot = entry * tiles + tile
                product(block_of(slot), pair_left[slot], tiles + slot)
        return carry

    def applied(turn, vec):
        build(vec, local, tiles)
        lax.fori_loop(0, tiles // 4, back_step, 0)
        back = [combined(1 + entry, shifts_of(shift_right, entry)) for entry in range(near)]
        spread = picked(
            hit_rows,
            [
                jnp.concatenate([back[entry][axis] for entry in range(near)], axis=0)
                for axis in range(3)
            ],
        )
        for axis in range(3):
            sent_f[turn, axis] = spread[axis][tiles:]
        copy_f(turn).start()
        field = combined(0, [local[axis] for axis in range(3)])
        field = [field[axis] + spread[axis][:tiles] for axis in range(3)]
        if turn == 0:
            ahead = [window[pl.ds(tiles * 8 + 3 + axis, tiles, stride=8), :] for axis in range(3)]
        else:
            copy_w(turn).wait_recv()
            ahead = [ahead_w[turn, axis] for axis in range(3)]
        window_vec = [jnp.concatenate([vec[axis], ahead[axis]], axis=0) for axis in range(3)]
        build(picked(hit_own, window_vec), local_far, slots)
        lax.fori_loop(0, tiles // 4, left_step, 0)
        for entry in range(near):
            more = combined(1 + entry, shifts_of(shift_left, entry))
            field = [field[axis] + more[axis] for axis in range(3)]
        copy_f(turn).wait_recv()
        return [vec[axis] * alpha_inv - (field[axis] + back_f[turn, axis]) for axis in range(3)]

    def dot_rows(left, right):
        total = left[0] * right[0] + left[1] * right[1] + left[2] * right[2]
        return jnp.sum(total, axis=0, keepdims=True)

    def send_dots(turn, resid, w):
        dots[turn, 0] = jnp.where(
            sub_ids == 0, dot_rows(resid, resid), jnp.where(sub_ids == 1, dot_rows(resid, w), 0.0)
        )

        def send(step, carry):
            pltpu.make_async_remote_copy(
                src_ref=dots.at[turn, 0],
                dst_ref=dots.at[turn, step],
                send_sem=dot_sem.at[0, turn],
                recv_sem=dot_sem.at[1, turn],
                device_id={"gx": lax.rem(me + step, count)},
                device_id_type=MESH,
            ).start()
            return carry

        lax.fori_loop(1, count, send, 0)

    def wait_dots(turn, which):
        whole = dots.at[turn, pl.ds(1, count - 1)]
        pltpu.make_async_copy(whole, whole, dot_sem.at[which, turn]).wait()

    resid = [window[pl.ds(3 + axis, tiles, stride=8), :] for axis in range(3)]
    w = applied(0, resid)
    solution = direction = s = z = None
    norm_last = step_last = None
    for turn in range(ITERS):
        more_turns = turn + 1 < ITERS
        if more_turns:
            for axis in range(3):
                sent_w[turn + 1, axis] = w[axis]
            copy_w(turn + 1).start()
        send_dots(turn, resid, w)
        if more_turns:
            q = applied(turn + 1, w)
        wait_dots(turn, 1)
        sums = jnp.sum(jnp.sum(dots[turn], axis=0), axis=1, keepdims=True)
        norm = sums[0:1, :]
        product_now = sums[1:2, :]
        if turn == 0:
            step = norm / product_now
            direction, s = resid, w
            solution = [step * direction[axis] for axis in range(3)]
            if more_turns:
                z = q
        else:
            ratio = norm / norm_last
            step = norm / (product_now - ratio * norm / step_last)
            direction = [resid[axis] + ratio * direction[axis] for axis in range(3)]
            s = [w[axis] + ratio * s[axis] for axis in range(3)]
            solution = [solution[axis] + step * direction[axis] for axis in range(3)]
            if more_turns:
                z = [q[axis] + ratio * z[axis] for axis in range(3)]
        resid = [resid[axis] - step * s[axis] for axis in range(3)]
        if more_turns:
            w = [w[axis] - step * z[axis] for axis in range(3)]
        norm_last, step_last = norm, step

    def put_final(row, value):
        out_ref[pl.ds(row, tiles, stride=8), :] = value

    for axis in range(3):
        put_final(axis, solution[axis])
        put_final(3 + axis, resid[axis])
    put_final(6, jnp.zeros((tiles, width), F32))
    put_final(7, jnp.zeros((tiles, width), F32))

    pack_copy.wait_send()
    for turn in range(ITERS):
        if turn > 0:
            copy_w(turn).wait_send()
        copy_f(turn).wait_send()
        wait_dots(turn, 0)


def on_device(positions, polar, field_ext, tile_atom, tile_list, image_shift):
    tiles, links = tile_list.shape
    atoms = tile_atom.shape[0]
    width = atoms // tiles
    near = links - 1
    count = lax.axis_size("gx")
    pairs = (2 * width, 2 * width)
    vmem = pl.BlockSpec(memory_space=pltpu.VMEM)
    smem = pl.BlockSpec(memory_space=pltpu.SMEM)
    out = jax.ShapeDtypeStruct((3, atoms), F32)
    vectors = pltpu.VMEM((ITERS, 3, tiles, width), F32)
    tiled = jax.ShapeDtypeStruct((tiles * 8, width), F32)
    window, inverse, hits, image = pl.pallas_call(
        functools.partial(tiling_kernel, tiles, links),
        out_shape=(
            tiled,
            jax.ShapeDtypeStruct((tiles, width), jnp.int32),
            jax.ShapeDtypeStruct((2 * near * tiles, width), F32),
            jax.ShapeDtypeStruct((3, near * tiles, width), F32),
        ),
        in_specs=[smem, smem, vmem, vmem, vmem, vmem],
        out_specs=(vmem, vmem, vmem, vmem),
        scratch_shapes=[pltpu.VMEM((tiles * 8, width), F32)],
    )(
        tile_list.reshape(-1),
        image_shift.reshape(-1),
        positions,
        polar.reshape(1, atoms),
        field_ext,
        tile_atom.reshape(tiles, width),
    )
    found = pl.pallas_call(
        functools.partial(kernel, count, tiles, links),
        out_shape=tiled,
        in_specs=[vmem, vmem, vmem],
        out_specs=vmem,
        scratch_shapes=[
            pltpu.VMEM((2 * tiles * 8, width), F32),
            pltpu.VMEM((tiles,) + pairs, BF16),
            pltpu.VMEM((near * tiles,) + pairs, BF16),
            pltpu.VMEM((near * tiles,) + pairs, BF16),
            pltpu.VMEM((near, width, width), F32),
            pltpu.VMEM((near, width, width), F32),
            pltpu.VMEM((near * tiles * 8, width), F32),
            pltpu.VMEM((3, tiles, width), F32),
            pltpu.VMEM((3, near * tiles, width), F32),
            pltpu.VMEM((3, near * tiles, width), F32),
            pltpu.VMEM((3, near * tiles, width), F32),
            pltpu.VMEM((near * tiles * ROWS, width), F32),
            pltpu.VMEM((near * tiles * ROWS, width), F32),
            pltpu.VMEM(((1 + near) * tiles * ROWS, width), F32),
            vectors,
            vectors,
            vectors,
            vectors,
            pltpu.VMEM((ITERS, count, 8, width), F32),
            pltpu.SemaphoreType.DMA((2,)),
            pltpu.SemaphoreType.DMA((2, ITERS)),
            pltpu.SemaphoreType.DMA((2, ITERS)),
            pltpu.SemaphoreType.DMA((2, ITERS)),
        ],
        compiler_params=pltpu.CompilerParams(collective_id=0, has_side_effects=True),
    )(window, hits, image)
    return pl.pallas_call(
        functools.partial(untiling_kernel, tiles),
        out_shape=(out, out),
        in_specs=[vmem, vmem],
        out_specs=(vmem, vmem),
    )(found, inverse)


def solution(mesh):
    in_specs = (
        P(None, ("rep", "gx")),
        P(("rep", "gx")),
        P(None, ("rep", "gx")),
        P(("rep", "gx")),
        P(("rep", "gx"), None),
        P(None, ("rep", "gx"), None),
    )
    out_specs = (P(None, ("rep", "gx")), P(None, ("rep", "gx")))
    return jax.shard_map(
        on_device, mesh=mesh, in_specs=in_specs, out_specs=out_specs, check_vma=False
    )
```

profile of v0, /device:TPU:0, one launch (start us, length us, event | category | flops | bytes accessed | tf_op | source)
XLA Modules:
  0.0 73.2 jit_solution(9993016525571853515)
XLA Ops:
  0.6 0.0 copy-start.1
  0.6 0.7 copy-done.1
  1.3 0.1 copy.9
  1.4 0.0 copy-start
  1.4 0.6 reshape.16.list_ref
  2.0 0.0 copy-done
  2.1 0.1 copy.10
  2.2 0.7 reshape.17.shift_ref
  2.9 5.3 %shard_map.77 = (f32[256,128]{1,0:T(8,128)}, s32[32,128]{1,0:T(8,128)}, f32[128,128]{1,0:T(8,128)}, f32[3,64,128]{2,1,0:T(8,128)}) custom-call(s32[96]{0:T(128)} %reshape.16.list_ref, s32[192]{0:T(256)} %reshape.17.shift_ref, f32[3,4096]{1,0:T(4,128)} %place_ref.1, f32[1,4096]{1,0:T(1,128)} %bitcast.2, f32[3,4096]{1,0:T(4,128)} %field_ref.1, s32[32,128]{1,0:T(8,128)} %bitcast.3), custom_call_target="tpu_custom_call" | custom-call | tf_op jit(solution)/shard_map/pallas_call | solution.py:507
  8.2 61.6 %shard_map.78.tiled_ref = f32[256,128]{1,0:T(8,128)} custom-call(f32[256,128]{1,0:T(8,128)} %get-tuple-element.6.tiled_ref, f32[128,128]{1,0:T(8,128)} %get-tuple-element.7.hits_ref, f32[3,64,128]{2,1,0:T(8,128)} %get-tuple-element.8.image_ref), custom_call_target="tpu_custom_call" | custom-call | tf_op jit(solution)/shard_map/pallas_call | solution.py:526
  69.8 3.3 %shard_map.79 = (f32[3,4096]{1,0:T(4,128)}, f32[3,4096]{1,0:T(4,128)}) custom-call(f32[256,128]{1,0:T(8,128)} %shard_map.78.tiled_ref, s32[32,128]{1,0:T(8,128)} %get-tuple-element.9.inverse), custom_call_target="tpu_custom_call" | custom-call | tf_op jit(solution)/shard_map/pallas_call | solution.py:558
Async XLA Ops:
  0.6 0.7 copy-start.1
  1.4 0.7 copy-start
where the time goes:
time: 73.4 us; the launch traced here: 73.2 us
  Pallas kernels  70.3 us (96%)
  local copies, waits for them, and re-layouts  2.24 us (3%)
    pallas_call x1, Pallas kernels, on_device(): pl.pallas_call(functools.partial(kernel, count, tiles, links), out_shape=...  61.6 us
    pallas_call x1, Pallas kernels, on_device(): pl.pallas_call(functools.partial(tiling_kernel, tiles, links), out_shape=...  5.32 us
    pallas_call x1, Pallas kernels, on_device(): pl.pallas_call(functools.partial(untiling_kernel, tiles), out_shape=(out,...  3.32 us

commit v1 on v0

v1 whole, which is shorter than its diff:
```python
import functools

import jax
import jax.numpy as jnp
from jax import lax
from jax.experimental import pallas as pl
from jax.experimental.pallas import tpu as pltpu
from jax.sharding import PartitionSpec as P

ITERS = 4
MESH = pl.DeviceIdType.MESH
thole_factor = 0.39
LN2 = 0.6931471805599453
AWAY = 1e28
F32 = jnp.float32
BF16 = jnp.bfloat16


def split_two(value):
    high = value.astype(BF16)
    return high, (value - high.astype(F32)).astype(BF16)


def split_three(value):
    high = value.astype(BF16)
    rest = value - high.astype(F32)
    middle = rest.astype(BF16)
    return high, middle, (rest - middle.astype(F32)).astype(BF16)


def gather_tile(row, source, tiles):
    width = 128
    inner = jnp.broadcast_to(row & (width - 1), (8, width))
    outer = jnp.broadcast_to(row >> 7, (8, width))
    value = jnp.zeros((8, width), F32)
    for tile in range(tiles):
        picked = jnp.take_along_axis(
            source[pl.ds(tile * 8, 8), :], inner, axis=1, mode="promise_in_bounds"
        )
        value = jnp.where(outer == tile, picked, value)
    return value


def tiling_kernel(tiles, place_ref, polar_ref, field_ref, atom_ref, out_ref, inverse, feat):
    width = 128
    for tile in range(tiles):
        lanes = pl.ds(tile * width, width)
        feat[tile * 8 : tile * 8 + 3, :] = place_ref[:, lanes]
        feat[tile * 8 + 3 : tile * 8 + 6, :] = field_ref[:, lanes]
        feat[tile * 8 + 6 : tile * 8 + 7, :] = polar_ref[:, lanes]
        feat[tile * 8 + 7 : tile * 8 + 8, :] = jnp.ones((1, width), F32)
    sub_ids = lax.broadcasted_iota(jnp.int32, (8, width), 0)

    def fill(tile, carry):
        value = gather_tile(atom_ref[pl.ds(tile, 1), :], feat, tiles)
        root = lax.rsqrt(value)
        value = jnp.where(sub_ids == 7, pltpu.roll(root, 1, 0), value)
        out_ref[pl.ds(pl.multiple_of(tile * 8, 8), 8), :] = value
        return carry

    lax.fori_loop(0, tiles, fill, 0, unroll=4)

    lane_ids = lax.broadcasted_iota(jnp.int32, (width, width), 0)
    tile_ids = lax.broadcasted_iota(jnp.int32, (tiles, width), 0)
    lane_row = lax.broadcasted_iota(jnp.int32, (tiles, width), 1).astype(F32)

    def invert(tile, total):
        row = atom_ref[pl.ds(tile, 1), :]
        outer = tile_ids == (row >> 7)
        number = jnp.full((tiles, width), tile, jnp.int32).astype(F32)
        left = jnp.concatenate(
            [jnp.where(outer, number, 0.0), jnp.where(outer, lane_row, 0.0)], axis=0
        ).astype(BF16)
        right = jnp.where(lane_ids == (row & (width - 1)), 1.0, 0.0).astype(BF16)
        return total + lax.dot_general(
            left, right, (((1,), (1,)), ((), ())), preferred_element_type=F32
        )

    found = lax.fori_loop(
        0, tiles, invert, jnp.zeros((2 * tiles, width), F32), unroll=4
    )
    inverse[...] = (found[:tiles] * float(width) + found[tiles:]).astype(jnp.int32)


def untiling_kernel(tiles, tiled_ref, inverse, dip_ref, res_ref):
    width = 128

    def give(tile, carry):
        value = gather_tile(inverse[pl.ds(tile, 1), :], tiled_ref, tiles)
        lanes = pl.ds(pl.multiple_of(tile * width, width), width)
        dip_ref[:, lanes] = value[0:3]
        res_ref[:, lanes] = value[3:6]
        return carry

    lax.fori_loop(0, tiles, give, 0, unroll=4)


def eight(index):
    return pl.ds(pl.multiple_of(index * 8, 8), 8)


def kernel(
    count,
    tiles,
    links,
    list_ref,
    shift_ref,
    names_ref,
    tiled_ref,
    out_ref,
    window,
    middle,
    placed,
    centred,
    local,
    away,
    pair_own,
    pair_back,
    pair_left,
    bases,
    coefs,
    vectors,
    blocks,
    fields,
    summed,
    sent_w,
    ahead_w,
    sent_f,
    back_f,
    dots,
    pack_sem,
    w_sem,
    f_sem,
    dot_sem,
):
    width = 128
    near = links - 1
    slots = near * tiles
    me = lax.axis_index("gx")
    after = lax.rem(me + 1, count)
    before = lax.rem(me + count - 1, count)

    barrier = pltpu.get_barrier_semaphore()

    def greet(step, carry):
        pl.semaphore_signal(
            barrier, inc=1, device_id={"gx": lax.rem(me + step, count)}, device_id_type=MESH
        )
        return carry

    lax.fori_loop(1, count, greet, 0)

    sub_ids = lax.broadcasted_iota(jnp.int32, (8, width), 0)
    low_rows = sub_ids < 4

    window[0 : tiles * 8, :] = tiled_ref[...]
    pl.semaphore_wait(barrier, count - 1)
    pack_copy = pltpu.make_async_remote_copy(
        src_ref=tiled_ref,
        dst_ref=window.at[pl.ds(tiles * 8, tiles * 8)],
        send_sem=pack_sem.at[0],
        recv_sem=pack_sem.at[1],
        device_id={"gx": before},
        device_id_type=MESH,
    )
    pack_copy.start()

    row_ids = lax.broadcasted_iota(jnp.int32, (width, width), 0)
    column_ids = lax.broadcasted_iota(jnp.int32, (width, width), 1)
    away[...] = jnp.where(row_ids == column_ids, AWAY, 0.0)

    def strided(first, row):
        return pl.ds(first * 8 + row, tiles, stride=8)

    def centre(first):
        whole = slice(first, first + tiles)
        ones = jnp.ones((tiles, width), F32)
        for axis in range(3):
            here = window[strided(first, axis), :]
            mean = jnp.floor(jnp.mean(here, axis=1, keepdims=True) + 0.5)
            mean = jnp.broadcast_to(mean, here.shape)
            middle[strided(first, axis), :] = mean
            here = here - mean
            local[axis, whole, :] = here
            bases[strided(first, axis), :] = here
            bases[strided(first, axis + 4), :] = here
        bases[strided(first, 3), :] = ones
        bases[strided(first, 7), :] = ones
        for row in range(3, 8):
            middle[strided(first, row), :] = jnp.zeros((tiles, width), F32)
        for tile in range(first, first + tiles):
            placed[tile] = window[tile * 8 : tile * 8 + 8, :]
            centred[tile] = middle[tile * 8 : tile * 8 + 8, :]

    def pair_rows(columns, other, factor, first, same):
        rows = slice(first, first + 16)
        off_x = other[0:1, :] - columns[rows, 0:1]
        off_y = other[1:2, :] - columns[rows, 1:2]
        off_z = other[2:3, :] - columns[rows, 2:3]
        dist_sq = off_x * off_x + off_y * off_y + off_z * off_z
        if same:
            dist_sq = dist_sq + away[rows, :]
        inv = lax.rsqrt(dist_sq)
        inv_sq = inv * inv
        inv_cube = inv_sq * inv
        cube = dist_sq * (dist_sq * inv)
        scale = columns[rows, 7:8] * factor
        decay = jnp.exp(-(scale * cube))
        three = inv_cube - inv_cube * decay
        five = inv_sq * (three - scale * decay)
        return three, five

    def store_pair(target, index, first, three, five):
        rows = slice(first, first + 16)
        more = slice(width + first, width + first + 16)
        high, low = split_two(five)
        target[index, rows, 0:width] = high
        target[index, rows, width : 2 * width] = low
        high, low = split_two(three)
        target[index, more, 0:width] = high
        target[index, more, width : 2 * width] = low

    def put_coefs(index, shift):
        def row(at):
            return jnp.broadcast_to(-shift[at : at + 1, :], (8, width))

        coefs[index, 0] = jnp.where(low_rows, row(0), 1.0)
        coefs[index, 1] = jnp.where(low_rows, row(1), row(2))
        coefs[index, 2] = shift

    def own_pairs(tile):
        here = window[eight(tile), :]
        columns = here.T
        factor = thole_factor * here[7:8, :]
        for first in range(0, width, 16):
            three, five = pair_rows(columns, here, factor, first, True)
            store_pair(pair_own, tile, first, three, five)
        put_coefs(tile, here - middle[eight(tile), :])

    def grouped(size, body):
        def step(group, carry):
            for offset in range(size):
                body(group * size + offset)
            return carry

        lax.fori_loop(0, tiles // size, step, 0)

    centre(0)
    grouped(2, own_pairs)

    pack_copy.wait_recv()
    centre(tiles)

    lengths = (jnp.where(me == count - 1, 4.0 * count, 0.0), 128.0, 2.0 * tiles)

    def far_pairs(tile):
        here = window[eight(tile), :]
        here_middle = middle[eight(tile), :]
        columns = here.T
        for entry in range(near):
            slot = entry * tiles + tile
            named = list_ref[entry + 1, tile]
            crossing = jnp.full((8, width), named, jnp.int32) >= tiles
            moves = jnp.where(
                sub_ids == 0,
                jnp.where(crossing, lengths[0], 0.0),
                jnp.where(
                    sub_ids == 1,
                    shift_ref[entry + 1, 0, tile].astype(F32) * lengths[1],
                    jnp.where(sub_ids == 2, shift_ref[entry + 1, 1, tile].astype(F32) * lengths[2], 0.0),
                ),
            )
            other = placed[named] + moves
            put_coefs(tiles + slot, other - here_middle)
            put_coefs(tiles + slots + slot, here - (centred[named] + moves))
            factor = thole_factor * other[7:8, :]
            for first in range(0, width, 16):
                three, five = pair_rows(columns, other, factor, first, False)
                store_pair(pair_back, slot, first, three, five)
            for part in (slice(0, width), slice(width, 2 * width)):
                for half in (slice(0, width), slice(width, 2 * width)):
                    pair_left[slot, part, half] = pair_back[slot, part, half].T

    grouped(1, far_pairs)

    named_row = jnp.concatenate(
        [names_ref[entry + 1 : entry + 2, :] for entry in range(near)] * 3, axis=1
    )
    window_ids = lax.broadcasted_iota(jnp.int32, (2 * tiles, 3 * slots), 0)
    hits = jnp.where(window_ids == named_row, 1.0, 0.0).astype(BF16)

    alpha_inv = 1.0 / window[strided(0, 6), :]

    def put_vector(first, vec):
        whole = slice(first, first + tiles)
        along = local[0, whole, :] * vec[0] + local[1, whole, :] * vec[1] + local[2, whole, :] * vec[2]
        for axis in range(3):
            vectors[strided(first, axis), :] = 3.0 * vec[axis]
            vectors[strided(first, axis + 4), :] = -vec[axis]
        vectors[strided(first, 3), :] = 3.0 * along

    vectors[...] = jnp.zeros_like(vectors)

    def make_block(tile):
        base = bases[eight(tile), :]
        vec = vectors[eight(tile), :]

        def row(at):
            return jnp.broadcast_to(vec[at : at + 1, :], (8, width))

        moments = jnp.concatenate(
            [
                base * jnp.where(low_rows, row(0), row(3)),
                base * jnp.where(low_rows, row(1), row(2)),
            ],
            axis=0,
        )
        minus = jnp.concatenate([jnp.where(low_rows, 0.0, vec), jnp.zeros((8, width), F32)], axis=0)
        for part, value in enumerate(split_three(moments)):
            blocks[tile, part * 16 : part * 16 + 16, 0:width] = value
        for part, value in enumerate(split_three(minus)):
            blocks[tile, part * 16 : part * 16 + 16, width : 2 * width] = value

    def product(tile, weights, index):
        out = jnp.dot(blocks[tile], weights, preferred_element_type=F32)
        out = out[:, :width] + out[:, width:]
        out = (out[0:16] + out[16:32]) + out[32:48]
        total = coefs[index, 0] * out[0:8] + coefs[index, 1] * out[8:16]
        total = total + pltpu.roll(total, 4, 0)
        return total - coefs[index, 2] * jnp.broadcast_to(total[3:4, :], (8, width))

    def copy_w(turn):
        return pltpu.make_async_remote_copy(
            src_ref=sent_w.at[turn],
            dst_ref=ahead_w.at[turn],
            send_sem=w_sem.at[0, turn],
            recv_sem=w_sem.at[1, turn],
            device_id={"gx": before},
            device_id_type=MESH,
        )

    def copy_f(turn):
        return pltpu.make_async_remote_copy(
            src_ref=sent_f.at[turn],
            dst_ref=back_f.at[turn],
            send_sem=f_sem.at[0, turn],
            recv_sem=f_sem.at[1, turn],
            device_id={"gx": after},
            device_id_type=MESH,
        )

    def back_step(tile):
        make_block(tile)
        for entry in range(near):
            slot = entry * tiles + tile
            fields[eight(slot), :] = product(tile, pair_back[slot], tiles + slot)

    def own_step(tile):
        summed[eight(tile), :] = product(tile, pair_own[tile], tile)

    def left_step(tile):
        total = summed[eight(tile), :]
        for entry in range(near):
            slot = entry * tiles + tile
            named = list_ref[entry + 1, tile]
            total = total + product(named, pair_left[slot], tiles + slots + slot)
        summed[eight(tile), :] = total

    def applied(turn, vec):
        put_vector(0, vec)
        grouped(8, back_step)
        back = jnp.concatenate(
            [fields[pl.ds(axis, slots, stride=8), :] for axis in range(3)], axis=1
        )
        spread = jnp.dot(
            hits, jnp.concatenate(split_three(back), axis=0), preferred_element_type=F32
        )
        for axis in range(3):
            sent_f[turn, axis] = spread[tiles:, axis * width : (axis + 1) * width]
        copy_f(turn).start()
        grouped(16, own_step)
        if turn == 0:
            ahead = [window[strided(tiles, 3 + axis), :] for axis in range(3)]
        else:
            copy_w(turn).wait_recv()
            ahead = [ahead_w[turn, axis] for axis in range(3)]
        put_vector(tiles, ahead)
        for tile in range(tiles):
            make_block(tiles + tile)
        grouped(8, left_step)
        field = [
            summed[strided(0, axis), :] + spread[:tiles, axis * width : (axis + 1) * width]
            for axis in range(3)
        ]
        copy_f(turn).wait_recv()
        return [vec[axis] * alpha_inv - (field[axis] + back_f[turn, axis]) for axis in range(3)]

    def dot_rows(left, right):
        total = left[0] * right[0] + left[1] * right[1] + left[2] * right[2]
        return jnp.sum(total, axis=0, keepdims=True)

    def send_dots(turn, resid, w):
        dots[turn, 0] = jnp.where(
            sub_ids == 0, dot_rows(resid, resid), jnp.where(sub_ids == 1, dot_rows(resid, w), 0.0)
        )

        def send(step, carry):
            pltpu.make_async_remote_copy(
                src_ref=dots.at[turn, 0],
                dst_ref=dots.at[turn, step],
                send_sem=dot_sem.at[0, turn],
                recv_sem=dot_sem.at[1, turn],
                device_id={"gx": lax.rem(me + step, count)},
                device_id_type=MESH,
            ).start()
            return carry

        lax.fori_loop(1, count, send, 0)

    def wait_dots(turn, which):
        whole = dots.at[turn, pl.ds(1, count - 1)]
        pltpu.make_async_copy(whole, whole, dot_sem.at[which, turn]).wait()

    resid = [window[strided(0, 3 + axis), :] for axis in range(3)]
    w = applied(0, resid)
    solution = direction = s = z = None
    norm_last = step_last = None
    for turn in range(ITERS):
        more_turns = turn + 1 < ITERS
        if more_turns:
            for axis in range(3):
                sent_w[turn + 1, axis] = w[axis]
            copy_w(turn + 1).start()
        send_dots(turn, resid, w)
        if more_turns:
            q = applied(turn + 1, w)
        wait_dots(turn, 1)
        sums = jnp.sum(jnp.sum(dots[turn], axis=0), axis=1, keepdims=True)
        norm = sums[0:1, :]
        product_now = sums[1:2, :]
        if turn == 0:
            step = norm / product_now
            direction, s = resid, w
            solution = [step * direction[axis] for axis in range(3)]
            if more_turns:
                z = q
        else:
            ratio = norm / norm_last
            step = norm / (product_now - ratio * norm / step_last)
            direction = [resid[axis] + ratio * direction[axis] for axis in range(3)]
            s = [w[axis] + ratio * s[axis] for axis in range(3)]
            solution = [solution[axis] + step * direction[axis] for axis in range(3)]
            if more_turns:
                z = [q[axis] + ratio * z[axis] for axis in range(3)]
        resid = [resid[axis] - step * s[axis] for axis in range(3)]
        if more_turns:
            w = [w[axis] - step * z[axis] for axis in range(3)]
        norm_last, step_last = norm, step

    for axis in range(3):
        out_ref[strided(0, axis), :] = solution[axis]
        out_ref[strided(0, 3 + axis), :] = resid[axis]
    out_ref[strided(0, 6), :] = jnp.zeros((tiles, width), F32)
    out_ref[strided(0, 7), :] = jnp.zeros((tiles, width), F32)

    pack_copy.wait_send()
    for turn in range(ITERS):
        if turn > 0:
            copy_w(turn).wait_send()
        copy_f(turn).wait_send()
        wait_dots(turn, 0)


def on_device(positions, polar, field_ext, tile_atom, tile_list, image_shift):
    tiles, links = tile_list.shape
    atoms = tile_atom.shape[0]
    width = atoms // tiles
    near = links - 1
    count = lax.axis_size("gx")
    pairs = (2 * width, 2 * width)
    vmem = pl.BlockSpec(memory_space=pltpu.VMEM)
    smem = pl.BlockSpec(memory_space=pltpu.SMEM)
    out = jax.ShapeDtypeStruct((3, atoms), F32)
    vectors = pltpu.VMEM((ITERS, 3, tiles, width), F32)
    tiled = jax.ShapeDtypeStruct((tiles * 8, width), F32)
    per_window = pltpu.VMEM((2 * tiles * 8, width), F32)
    window, inverse = pl.pallas_call(
        functools.partial(tiling_kernel, tiles),
        out_shape=(tiled, jax.ShapeDtypeStruct((tiles, width), jnp.int32)),
        in_specs=[vmem, vmem, vmem, vmem],
        out_specs=(vmem, vmem),
        scratch_shapes=[pltpu.VMEM((tiles * 8, width), F32)],
    )(positions, polar.reshape(1, atoms), field_ext, tile_atom.reshape(tiles, width))
    names = tile_list.T
    found = pl.pallas_call(
        functools.partial(kernel, count, tiles, links),
        out_shape=tiled,
        in_specs=[smem, smem, vmem, vmem],
        out_specs=vmem,
        scratch_shapes=[
            per_window,
            per_window,
            pltpu.VMEM((2 * tiles, 8, width), F32),
            pltpu.VMEM((2 * tiles, 8, width), F32),
            pltpu.VMEM((3, 2 * tiles, width), F32),
            pltpu.VMEM((width, width), F32),
            pltpu.VMEM((tiles,) + pairs, BF16),
            pltpu.VMEM((near * tiles,) + pairs, BF16),
            pltpu.VMEM((near * tiles,) + pairs, BF16),
            per_window,
            pltpu.VMEM(((1 + 2 * near) * tiles, 3, 8, width), F32),
            per_window,
            pltpu.VMEM((2 * tiles, 48, 2 * width), BF16),
            pltpu.VMEM((near * tiles * 8, width), F32),
            pltpu.VMEM((tiles * 8, width), F32),
            vectors,
            vectors,
            vectors,
            vectors,
            pltpu.VMEM((ITERS, count, 8, width), F32),
            pltpu.SemaphoreType.DMA((2,)),
            pltpu.SemaphoreType.DMA((2, ITERS)),
            pltpu.SemaphoreType.DMA((2, ITERS)),
            pltpu.SemaphoreType.DMA((2, ITERS)),
        ],
        compiler_params=pltpu.CompilerParams(collective_id=0, has_side_effects=True),
    )(names, image_shift.transpose(2, 0, 1), names, window)
    return pl.pallas_call(
        functools.partial(untiling_kernel, tiles),
        out_shape=(out, out),
        in_specs=[vmem, vmem],
        out_specs=(vmem, vmem),
    )(found, inverse)


def solution(mesh):
    in_specs = (
        P(None, ("rep", "gx")),
        P(("rep", "gx")),
        P(None, ("rep", "gx")),
        P(("rep", "gx")),
        P(("rep", "gx"), None),
        P(None, ("rep", "gx"), None),
    )
    out_specs = (P(None, ("rep", "gx")), P(None, ("rep", "gx")))
    return jax.shard_map(
        on_device, mesh=mesh, in_specs=in_specs, out_specs=out_specs, check_vma=False
    )
```

time: 73.4 us -> 65.8 us (0.90)
  Pallas kernels: 70.3 us -> 64.9 us
  local copies, waits for them, and re-layouts: 2.24 us -> 0 us
    pallas_call x1, Pallas kernels: 61.6 us -> 56.6 us  [on_device(): pl.pallas_call(functools.partial(kernel, count, tiles, links), out_shape=...]
    reshape x2 -> x0, local copies, waits for them, and re-layouts: 1.35 us -> none  [the longest x1 0.7 us: on_device(): image_shift.reshape(-1)]
    unnamed x6 -> x0, local copies, waits for them, and re-layouts: 0.9 us -> none
where the time goes in v1:
time: 65.8 us; the launch traced here: 65.6 us
  Pallas kernels  64.9 us (99%)
    pallas_call x1, Pallas kernels, on_device(): pl.pallas_call(functools.partial(kernel, count, tiles, links), out_shape=...  56.6 us
    pallas_call x1, Pallas kernels, on_device(): pl.pallas_call(functools.partial(tiling_kernel, tiles), out_shape=(tiled,...  4.95 us
    pallas_call x1, Pallas kernels, on_device(): pl.pallas_call(functools.partial(untiling_kernel, tiles), out_shape=(out,...  3.32 us

profile of v1, /device:TPU:0, one launch (start us, length us, event | category | flops | bytes accessed | tf_op | source)
XLA Modules:
  0.0 65.6 jit_solution(8798288574266273974)
XLA Ops:
  0.6 5.0 %shard_map.77 = (f32[256,128]{1,0:T(8,128)}, s32[32,128]{1,0:T(8,128)}) custom-call(f32[3,4096]{1,0:T(4,128)} %place_ref.1, f32[1,4096]{1,0:T(1,128)} %bitcast.4, f32[3,4096]{1,0:T(4,128)} %field_ref.1, s32[32,128]{1,0:T(8,128)} %bitcast.5), custom_call_target="tpu_custom_call" | custom-call | tf_op jit(solution)/shard_map/pallas_call | solution.py:487
  5.6 56.6 %shard_map.78.tiled_ref = f32[256,128]{1,0:T(8,128)} custom-call(s32[3,32]{1,0:T(4,128)} %bitcast.6, s32[3,2,32]{2,1,0:T(2,128)} %bitcast.8, s32[3,32]{1,0:T(4,128)} %bitcast.7, f32[256,128]{1,0:T(8,128)} %get-tuple-element.4.tiled_ref), custom_call_target="tpu_custom_call" | custom-call | tf_op jit(solution)/shard_map/pallas_call | solution.py:495
  62.2 3.3 %shard_map.79 = (f32[3,4096]{1,0:T(4,128)}, f32[3,4096]{1,0:T(4,128)}) custom-call(f32[256,128]{1,0:T(8,128)} %shard_map.78.tiled_ref, s32[32,128]{1,0:T(8,128)} %get-tuple-element.5.inverse), custom_call_target="tpu_custom_call" | custom-call | tf_op jit(solution)/shard_map/pallas_call | solution.py:528

commit v2 on v1

--- a/solution.py
+++ b/solution.py
@@ -189,14 +189,47 @@
         for row in range(3, 8):
             middle[strided(first, row), :] = jnp.zeros((tiles, width), F32)
         for tile in range(first, first + tiles):
-            placed[tile] = window[tile * 8 : tile * 8 + 8, :]
+            here = window[tile * 8 : tile * 8 + 8, :]
+            root = jnp.broadcast_to(here[7:8, :], (8, width))
+            placed[tile] = jnp.where(sub_ids < 3, here, jnp.where(sub_ids < 5, 0.0, root))
             centred[tile] = middle[tile * 8 : tile * 8 + 8, :]
 
-    def pair_rows(columns, other, factor, first, same):
+    def split_rows(value):
+        high = value.astype(BF16).astype(F32)
+        rest = value - high
+        middle = rest.astype(BF16).astype(F32)
+        return high, middle, rest - middle
+
+    def left_rows(tile):
+        ones = jnp.ones((24, width), F32)
+        return jnp.concatenate([*split_rows(placed[tile]), ones], axis=0).astype(BF16)
+
+    def right_rows(other):
+        high, mid, low = split_rows(jnp.where(sub_ids >= 5, other * -thole_factor, other))
+        zero = jnp.zeros((8, width), F32)
+        parts = []
+        for axis in range(3):
+            here = sub_ids == axis
+            one = jnp.where(here, -1.0, 0.0)
+            parts.append(
+                [one, one, one] + [jnp.where(here, value, 0.0) for value in (high, mid, low)]
+            )
+        third = jnp.where(sub_ids == 7, high, 0.0)
+        second = jnp.where(sub_ids == 6, mid, third)
+        parts.append([jnp.where(sub_ids == 5, low, second), second, third, zero, zero, zero])
+        parts = [jnp.concatenate(part, axis=0) for part in parts]
+        return jnp.concatenate(parts, axis=1).astype(BF16)
+
+    def offsets(left, right):
+        return lax.dot_general(
+            left, right, (((0,), (0,)), ((), ())), preferred_element_type=F32
+        )
+
+    def pair_rows(found, first, same):
         rows = slice(first, first + 16)
-        off_x = other[0:1, :] - columns[rows, 0:1]
-        off_y = other[1:2, :] - columns[rows, 1:2]
-        off_z = other[2:3, :] - columns[rows, 2:3]
+        off_x, off_y, off_z, scale = [
+            found[rows, part * width : (part + 1) * width] for part in range(4)
+        ]
         dist_sq = off_x * off_x + off_y * off_y + off_z * off_z
         if same:
             dist_sq = dist_sq + away[rows, :]
@@ -204,10 +237,9 @@
         inv_sq = inv * inv
         inv_cube = inv_sq * inv
         cube = dist_sq * (dist_sq * inv)
-        scale = columns[rows, 7:8] * factor
-        decay = jnp.exp(-(scale * cube))
+        decay = jnp.exp(scale * cube)
         three = inv_cube - inv_cube * decay
-        five = inv_sq * (three - scale * decay)
+        five = inv_sq * (three + scale * decay)
         return three, five
 
     def store_pair(target, index, first, three, five):
@@ -229,13 +261,12 @@
         coefs[index, 2] = shift
 
     def own_pairs(tile):
-        here = window[eight(tile), :]
-        columns = here.T
-        factor = thole_factor * here[7:8, :]
+        here = placed[tile]
+        found = offsets(left_rows(tile), right_rows(here))
         for first in range(0, width, 16):
-            three, five = pair_rows(columns, here, factor, first, True)
+            three, five = pair_rows(found, first, True)
             store_pair(pair_own, tile, first, three, five)
-        put_coefs(tile, here - middle[eight(tile), :])
+        put_coefs(tile, here - centred[tile])
 
     def grouped(size, body):
         def step(group, carry):
@@ -246,7 +277,7 @@
         lax.fori_loop(0, tiles // size, step, 0)
 
     centre(0)
-    grouped(2, own_pairs)
+    grouped(8, own_pairs)
 
     pack_copy.wait_recv()
     centre(tiles)
@@ -254,9 +285,9 @@
     lengths = (jnp.where(me == count - 1, 4.0 * count, 0.0), 128.0, 2.0 * tiles)
 
     def far_pairs(tile):
-        here = window[eight(tile), :]
-        here_middle = middle[eight(tile), :]
-        columns = here.T
+        here = placed[tile]
+        here_middle = centred[tile]
+        left = left_rows(tile)
         for entry in range(near):
             slot = entry * tiles + tile
             named = list_ref[entry + 1, tile]
@@ -273,15 +304,15 @@
             other = placed[named] + moves
             put_coefs(tiles + slot, other - here_middle)
             put_coefs(tiles + slots + slot, here - (centred[named] + moves))
-            factor = thole_factor * other[7:8, :]
+            found = offsets(left, right_rows(other))
             for first in range(0, width, 16):
-                three, five = pair_rows(columns, other, factor, first, False)
+                three, five = pair_rows(found, first, False)
                 store_pair(pair_back, slot, first, three, five)
             for part in (slice(0, width), slice(width, 2 * width)):
                 for half in (slice(0, width), slice(width, 2 * width)):
                     pair_left[slot, part, half] = pair_back[slot, part, half].T
 
-    grouped(1, far_pairs)
+    grouped(4, far_pairs)
 
     named_row = jnp.concatenate(
         [names_ref[entry + 1 : entry + 2, :] for entry in range(near)] * 3, axis=1
@@ -368,7 +399,7 @@
 
     def applied(turn, vec):
         put_vector(0, vec)
-        grouped(8, back_step)
+        grouped(16, back_step)
         back = jnp.concatenate(
             [fields[pl.ds(axis, slots, stride=8), :] for axis in range(3)], axis=1
         )
@@ -378,7 +409,7 @@
         for axis in range(3):
             sent_f[turn, axis] = spread[tiles:, axis * width : (axis + 1) * width]
         copy_f(turn).start()
-        grouped(16, own_step)
+        grouped(32, own_step)
         if turn == 0:
             ahead = [window[strided(tiles, 3 + axis), :] for axis in range(3)]
         else:
@@ -387,7 +418,7 @@
         put_vector(tiles, ahead)
         for tile in range(tiles):
             make_block(tiles + tile)
-        grouped(8, left_step)
+        grouped(16, left_step)
         field = [
             summed[strided(0, axis), :] + spread[:tiles, axis * width : (axis + 1) * width]
             for axis in range(3)

time: 65.8 us -> 57.8 us (0.88)
  Pallas kernels: 64.9 us -> 57 us
    pallas_call x1, Pallas kernels: 56.6 us -> 48.7 us  [on_device(): pl.pallas_call(functools.partial(kernel, count, tiles, links), out_shape=...]
where the time goes in v2:
time: 57.8 us; the launch traced here: 57.6 us
  Pallas kernels  57 us (99%)
  between operations  0.64 us (1%)
    pallas_call x1, Pallas kernels, on_device(): pl.pallas_call(functools.partial(kernel, count, tiles, links), out_shape=...  48.7 us
    pallas_call x1, Pallas kernels, on_device(): pl.pallas_call(functools.partial(tiling_kernel, tiles), out_shape=(tiled,...  4.95 us
    pallas_call x1, Pallas kernels, on_device(): pl.pallas_call(functools.partial(untiling_kernel, tiles), out_shape=(out,...  3.32 us

profile of v2, /device:TPU:0, one launch (start us, length us, event | category | flops | bytes accessed | tf_op | source)
XLA Modules:
  0.0 57.6 jit_solution(13897864220833638265)
XLA Ops:
  0.6 5.0 %shard_map.77 = (f32[256,128]{1,0:T(8,128)}, s32[32,128]{1,0:T(8,128)}) custom-call(f32[3,4096]{1,0:T(4,128)} %place_ref.1, f32[1,4096]{1,0:T(1,128)} %bitcast.4, f32[3,4096]{1,0:T(4,128)} %field_ref.1, s32[32,128]{1,0:T(8,128)} %bitcast.5), custom_call_target="tpu_custom_call" | custom-call | tf_op jit(solution)/shard_map/pallas_call | solution.py:518
  5.6 48.7 %shard_map.78.tiled_ref = f32[256,128]{1,0:T(8,128)} custom-call(s32[3,32]{1,0:T(4,128)} %bitcast.6, s32[3,2,32]{2,1,0:T(2,128)} %bitcast.8, s32[3,32]{1,0:T(4,128)} %bitcast.7, f32[256,128]{1,0:T(8,128)} %get-tuple-element.4.tiled_ref), custom_call_target="tpu_custom_call" | custom-call | tf_op jit(solution)/shard_map/pallas_call | solution.py:526
  54.3 3.3 %shard_map.79 = (f32[3,4096]{1,0:T(4,128)}, f32[3,4096]{1,0:T(4,128)}) custom-call(f32[256,128]{1,0:T(8,128)} %shard_map.78.tiled_ref, s32[32,128]{1,0:T(8,128)} %get-tuple-element.5.inverse), custom_call_target="tpu_custom_call" | custom-call | tf_op jit(solution)/shard_map/pallas_call | solution.py:559

commit v3 on v2

--- a/solution.py
+++ b/solution.py
@@ -41,60 +41,6 @@
     return value
 
 
-def tiling_kernel(tiles, place_ref, polar_ref, field_ref, atom_ref, out_ref, inverse, feat):
-    width = 128
-    for tile in range(tiles):
-        lanes = pl.ds(tile * width, width)
-        feat[tile * 8 : tile * 8 + 3, :] = place_ref[:, lanes]
-        feat[tile * 8 + 3 : tile * 8 + 6, :] = field_ref[:, lanes]
-        feat[tile * 8 + 6 : tile * 8 + 7, :] = polar_ref[:, lanes]
-        feat[tile * 8 + 7 : tile * 8 + 8, :] = jnp.ones((1, width), F32)
-    sub_ids = lax.broadcasted_iota(jnp.int32, (8, width), 0)
-
-    def fill(tile, carry):
-        value = gather_tile(atom_ref[pl.ds(tile, 1), :], feat, tiles)
-        root = lax.rsqrt(value)
-        value = jnp.where(sub_ids == 7, pltpu.roll(root, 1, 0), value)
-        out_ref[pl.ds(pl.multiple_of(tile * 8, 8), 8), :] = value
-        return carry
-
-    lax.fori_loop(0, tiles, fill, 0, unroll=4)
-
-    lane_ids = lax.broadcasted_iota(jnp.int32, (width, width), 0)
-    tile_ids = lax.broadcasted_iota(jnp.int32, (tiles, width), 0)
-    lane_row = lax.broadcasted_iota(jnp.int32, (tiles, width), 1).astype(F32)
-
-    def invert(tile, total):
-        row = atom_ref[pl.ds(tile, 1), :]
-        outer = tile_ids == (row >> 7)
-        number = jnp.full((tiles, width), tile, jnp.int32).astype(F32)
-        left = jnp.concatenate(
-            [jnp.where(outer, number, 0.0), jnp.where(outer, lane_row, 0.0)], axis=0
-        ).astype(BF16)
-        right = jnp.where(lane_ids == (row & (width - 1)), 1.0, 0.0).astype(BF16)
-        return total + lax.dot_general(
-            left, right, (((1,), (1,)), ((), ())), preferred_element_type=F32
-        )
-
-    found = lax.fori_loop(
-        0, tiles, invert, jnp.zeros((2 * tiles, width), F32), unroll=4
-    )
-    inverse[...] = (found[:tiles] * float(width) + found[tiles:]).astype(jnp.int32)
-
-
-def untiling_kernel(tiles, tiled_ref, inverse, dip_ref, res_ref):
-    width = 128
-
-    def give(tile, carry):
-        value = gather_tile(inverse[pl.ds(tile, 1), :], tiled_ref, tiles)
-        lanes = pl.ds(pl.multiple_of(tile * width, width), width)
-        dip_ref[:, lanes] = value[0:3]
-        res_ref[:, lanes] = value[3:6]
-        return carry
-
-    lax.fori_loop(0, tiles, give, 0, unroll=4)
-
-
 def eight(index):
     return pl.ds(pl.multiple_of(index * 8, 8), 8)
 
@@ -106,8 +52,16 @@
     list_ref,
     shift_ref,
     names_ref,
-    tiled_ref,
-    out_ref,
+    place_ref,
+    polar_ref,
+    field_ref,
+    atom_ref,
+    dip_ref,
+    res_ref,
+    feat,
+    inverse,
+    final,
+    found_ref,
     window,
     middle,
     placed,
@@ -123,6 +77,8 @@
     blocks,
     fields,
     summed,
+    sent_p,
+    ahead_p,
     sent_w,
     ahead_w,
     sent_f,
@@ -153,24 +109,64 @@
     sub_ids = lax.broadcasted_iota(jnp.int32, (8, width), 0)
     low_rows = sub_ids < 4
 
-    window[0 : tiles * 8, :] = tiled_ref[...]
+    def strided(first, row):
+        return pl.ds(first * 8 + row, tiles, stride=8)
+
+    def grouped(size, body):
+        def step(group, carry):
+            for offset in range(size):
+                body(group * size + offset)
+            return carry
+
+        lax.fori_loop(0, tiles // size, step, 0)
+
+    for tile in range(tiles):
+        lanes = pl.ds(tile * width, width)
+        feat[tile * 8 : tile * 8 + 3, :] = place_ref[:, lanes]
+        feat[tile * 8 + 3 : tile * 8 + 6, :] = field_ref[:, lanes]
+        feat[tile * 8 + 6 : tile * 8 + 7, :] = polar_ref[:, lanes]
+        feat[tile * 8 + 7 : tile * 8 + 8, :] = jnp.ones((1, width), F32)
+
+    def fill(tile):
+        value = gather_tile(atom_ref[pl.ds(tile, 1), :], feat, tiles)
+        root = lax.rsqrt(value)
+        window[eight(tile), :] = jnp.where(sub_ids == 7, pltpu.roll(root, 1, 0), value)
+
+    grouped(8, fill)
+
+    def copy_p():
+        return pltpu.make_async_remote_copy(
+            src_ref=sent_p,
+            dst_ref=ahead_p,
+            send_sem=pack_sem.at[0],
+            recv_sem=pack_sem.at[1],
+            device_id={"gx": before},
+            device_id_type=MESH,
+        )
+
+    def copy_w(turn):
+        return pltpu.make_async_remote_copy(
+            src_ref=sent_w.at[turn],
+            dst_ref=ahead_w.at[turn],
+            send_sem=w_sem.at[0, turn],
+            recv_sem=w_sem.at[1, turn],
+            device_id={"gx": before},
+            device_id_type=MESH,
+        )
+
+    pair_inputs = (0, 1, 2, 7)
+    for at, row in enumerate(pair_inputs):
+        sent_p[at] = window[strided(0, row), :]
+    resid = [window[strided(0, 3 + axis), :] for axis in range(3)]
+    for axis in range(3):
+        sent_w[0, axis] = resid[axis]
     pl.semaphore_wait(barrier, count - 1)
-    pack_copy = pltpu.make_async_remote_copy(
-        src_ref=tiled_ref,
-        dst_ref=window.at[pl.ds(tiles * 8, tiles * 8)],
-        send_sem=pack_sem.at[0],
-        recv_sem=pack_sem.at[1],
-        device_id={"gx": before},
-        device_id_type=MESH,
-    )
-    pack_copy.start()
+    copy_p().start()
+    copy_w(0).start()
 
     row_ids = lax.broadcasted_iota(jnp.int32, (width, width), 0)
     column_ids = lax.broadcasted_iota(jnp.int32, (width, width), 1)
     away[...] = jnp.where(row_ids == column_ids, AWAY, 0.0)
-
-    def strided(first, row):
-        return pl.ds(first * 8 + row, tiles, stride=8)
 
     def centre(first):
         whole = slice(first, first + tiles)
@@ -268,18 +264,39 @@
             store_pair(pair_own, tile, first, three, five)
         put_coefs(tile, here - centred[tile])
 
-    def grouped(size, body):
-        def step(group, carry):
-            for offset in range(size):
-                body(group * size + offset)
-            return carry
-
-        lax.fori_loop(0, tiles // size, step, 0)
-
     centre(0)
     grouped(8, own_pairs)
 
-    pack_copy.wait_recv()
+    lane_ids = row_ids
+    tile_ids = lax.broadcasted_iota(jnp.int32, (tiles, width), 0)
+    lane_row = lax.broadcasted_iota(jnp.int32, (tiles, width), 1).astype(F32)
+    found_ref[...] = jnp.zeros_like(found_ref)
+
+    def invert(tile):
+        row = atom_ref[pl.ds(tile, 1), :]
+        outer = tile_ids == (row >> 7)
+        number = jnp.full((tiles, width), tile, jnp.int32).astype(F32)
+        left = jnp.concatenate(
+            [jnp.where(outer, number, 0.0), jnp.where(outer, lane_row, 0.0)], axis=0
+        ).astype(BF16)
+        right = jnp.where(lane_ids == (row & (width - 1)), 1.0, 0.0).astype(BF16)
+        return lax.dot_general(
+            left, right, (((1,), (1,)), ((), ())), preferred_element_type=F32
+        )
+
+    def invert_step(group, carry):
+        total = found_ref[...]
+        for offset in range(8):
+            total = total + invert(group * 8 + offset)
+        found_ref[...] = total
+        return carry
+
+    lax.fori_loop(0, tiles // 8, invert_step, 0)
+    inverse[...] = (found_ref[:tiles] * float(width) + found_ref[tiles:]).astype(jnp.int32)
+
+    copy_p().wait_recv()
+    for at, row in enumerate(pair_inputs):
+        window[strided(tiles, row), :] = ahead_p[at]
     centre(tiles)
 
     lengths = (jnp.where(me == count - 1, 4.0 * count, 0.0), 128.0, 2.0 * tiles)
@@ -360,16 +377,6 @@
         total = total + pltpu.roll(total, 4, 0)
         return total - coefs[index, 2] * jnp.broadcast_to(total[3:4, :], (8, width))
 
-    def copy_w(turn):
-        return pltpu.make_async_remote_copy(
-            src_ref=sent_w.at[turn],
-            dst_ref=ahead_w.at[turn],
-            send_sem=w_sem.at[0, turn],
-            recv_sem=w_sem.at[1, turn],
-            device_id={"gx": before},
-            device_id_type=MESH,
-        )
-
     def copy_f(turn):
         return pltpu.make_async_remote_copy(
             src_ref=sent_f.at[turn],
@@ -410,11 +417,8 @@
             sent_f[turn, axis] = spread[tiles:, axis * width : (axis + 1) * width]
         copy_f(turn).start()
         grouped(32, own_step)
-        if turn == 0:
-            ahead = [window[strided(tiles, 3 + axis), :] for axis in range(3)]
-        else:
-            copy_w(turn).wait_recv()
-            ahead = [ahead_w[turn, axis] for axis in range(3)]
+        copy_w(turn).wait_recv()
+        ahead = [ahead_w[turn, axis] for axis in range(3)]
         put_vector(tiles, ahead)
         for tile in range(tiles):
             make_block(tiles + tile)
@@ -452,7 +456,6 @@
         whole = dots.at[turn, pl.ds(1, count - 1)]
         pltpu.make_async_copy(whole, whole, dot_sem.at[which, turn]).wait()
 
-    resid = [window[strided(0, 3 + axis), :] for axis in range(3)]
     w = applied(0, resid)
     solution = direction = s = z = None
     norm_last = step_last = None
@@ -489,15 +492,20 @@
         norm_last, step_last = norm, step
 
     for axis in range(3):
-        out_ref[strided(0, axis), :] = solution[axis]
-        out_ref[strided(0, 3 + axis), :] = resid[axis]
-    out_ref[strided(0, 6), :] = jnp.zeros((tiles, width), F32)
-    out_ref[strided(0, 7), :] = jnp.zeros((tiles, width), F32)
-
-    pack_copy.wait_send()
+        final[strided(0, axis), :] = solution[axis]
+        final[strided(0, 3 + axis), :] = resid[axis]
+
+    def give(tile):
+        value = gather_tile(inverse[pl.ds(tile, 1), :], final, tiles)
+        lanes = pl.ds(pl.multiple_of(tile * width, width), width)
+        dip_ref[:, lanes] = value[0:3]
+        res_ref[:, lanes] = value[3:6]
+
+    grouped(8, give)
+
+    copy_p().wait_send()
     for turn in range(ITERS):
-        if turn > 0:
-            copy_w(turn).wait_send()
+        copy_w(turn).wait_send()
         copy_f(turn).wait_send()
         wait_dots(turn, 0)
 
@@ -513,22 +521,19 @@
     smem = pl.BlockSpec(memory_space=pltpu.SMEM)
     out = jax.ShapeDtypeStruct((3, atoms), F32)
     vectors = pltpu.VMEM((ITERS, 3, tiles, width), F32)
-    tiled = jax.ShapeDtypeStruct((tiles * 8, width), F32)
+    per_slab = pltpu.VMEM((tiles * 8, width), F32)
     per_window = pltpu.VMEM((2 * tiles * 8, width), F32)
-    window, inverse = pl.pallas_call(
-        functools.partial(tiling_kernel, tiles),
-        out_shape=(tiled, jax.ShapeDtypeStruct((tiles, width), jnp.int32)),
-        in_specs=[vmem, vmem, vmem, vmem],
+    names = tile_list.T
+    return pl.pallas_call(
+        functools.partial(kernel, count, tiles, links),
+        out_shape=(out, out),
+        in_specs=[smem, smem, vmem, vmem, vmem, vmem, vmem],
         out_specs=(vmem, vmem),
-        scratch_shapes=[pltpu.VMEM((tiles * 8, width), F32)],
-    )(positions, polar.reshape(1, atoms), field_ext, tile_atom.reshape(tiles, width))
-    names = tile_list.T
-    found = pl.pallas_call(
-        functools.partial(kernel, count, tiles, links),
-        out_shape=tiled,
-        in_specs=[smem, smem, vmem, vmem],
-        out_specs=vmem,
         scratch_shapes=[
+            per_slab,
+            pltpu.VMEM((tiles, width), jnp.int32),
+            per_slab,
+            pltpu.VMEM((2 * tiles, width), F32),
             per_window,
             per_window,
             pltpu.VMEM((2 * tiles, 8, width), F32),
@@ -543,7 +548,9 @@
             per_window,
             pltpu.VMEM((2 * tiles, 48, 2 * width), BF16),
             pltpu.VMEM((near * tiles * 8, width), F32),
-            pltpu.VMEM((tiles * 8, width), F32),
+            per_slab,
+            pltpu.VMEM((4, tiles, width), F32),
+            pltpu.VMEM((4, tiles, width), F32),
             vectors,
             vectors,
             vectors,
@@ -555,13 +562,15 @@
             pltpu.SemaphoreType.DMA((2, ITERS)),
         ],
         compiler_params=pltpu.CompilerParams(collective_id=0, has_side_effects=True),
-    )(names, image_shift.transpose(2, 0, 1), names, window)
-    return pl.pallas_call(
-        functools.partial(untiling_kernel, tiles),
-        out_shape=(out, out),
-        in_specs=[vmem, vmem],
-        out_specs=(vmem, vmem),
-    )(found, inverse)
+    )(
+        names,
+        image_shift.transpose(2, 0, 1),
+        names,
+        positions,
+        polar.reshape(1, atoms),
+        field_ext,
+        tile_atom.reshape(tiles, width),
+    )
 
 
 def solution(mesh):

time: 57.8 us -> 51.9 us (0.90)
  Pallas kernels: 57 us -> 48.9 us
  local copies, waits for them, and re-layouts: 0 us -> 2.15 us
    pallas_call x2 -> x0, Pallas kernels: 8.27 us -> none  [the longest x1 4.95 us: on_device(): pl.pallas_call(functools.partial(tiling_kernel, tiles), out_shape=(tiled,...]
    unnamed x0 -> x4, local copies, waits for them, and re-layouts: none -> 2.15 us
where the time goes in v3:
time: 51.9 us; the launch traced here: 51.7 us
  Pallas kernels  48.9 us (94%)
  local copies, waits for them, and re-layouts  2.15 us (4%)
  between operations  0.65 us (1%)
    pallas_call x1, Pallas kernels, on_device(): pl.pallas_call(functools.partial(kernel, count, tiles, links), out_shape=...  48.9 us
    unnamed x4, local copies, waits for them, and re-layouts  2.15 us

profile of v3, /device:TPU:0, one launch (start us, length us, event | category | flops | bytes accessed | tf_op | source)
XLA Modules:
  0.0 51.7 jit_solution(13872779541391207567)
XLA Ops:
  0.6 48.9 %shard_map.77 = (f32[3,4096]{1,0:T(4,128)}, f32[3,4096]{1,0:T(4,128)}) custom-call(s32[3,32]{1,0:T(4,128)} %bitcast.6, s32[3,2,32]{2,1,0:T(2,128)} %bitcast.8, s32[3,32]{1,0:T(4,128)} %bitcast.7, f32[3,4096]{1,0:T(4,128)} %place_ref.1, f32[1,4096]{1,0:T(1,128)} %bitcast.4, f32[3,4096]{1,0:T(4,128)} %field_ref.1, s32[32,128]{1,0:T(8,128)} %bitcast.5), custom_call_target="tpu_custom_call" | custom-call | tf_op jit(solution)/shard_map/pallas_call | solution.py:527
  49.5 0.0 copy-start
  49.6 1.5 %copy.10 = f32[3,4096]{1,0:T(4,128)} copy(f32[3,4096]{1,0:T(4,128)} %get-tuple-element.4) | data formatting | bytes 98304
  51.1 0.0 copy-done
  51.1 0.6 %copy.11 = f32[3,4096]{1,0:T(4,128)} copy(f32[3,4096]{1,0:T(4,128)S(1)} %copy-done) | data formatting | bytes 98304
Async XLA Ops:
  49.5 1.5 %copy-start = (f32[3,4096]{1,0:T(4,128)S(1)}, f32[3,4096]{1,0:T(4,128)}, u32[]{:S(2)}) copy-start(f32[3,4096]{1,0:T(4,128)} %get-tuple-element.5) | copy-start | bytes 147460

commit v4 on v3

--- a/solution.py
+++ b/solution.py
@@ -28,14 +28,14 @@
     return high, middle, (rest - middle.astype(F32)).astype(BF16)
 
 
-def gather_tile(row, source, tiles):
+def gather_tile(row, source, tiles, first=0):
     width = 128
     inner = jnp.broadcast_to(row & (width - 1), (8, width))
     outer = jnp.broadcast_to(row >> 7, (8, width))
     value = jnp.zeros((8, width), F32)
     for tile in range(tiles):
         picked = jnp.take_along_axis(
-            source[pl.ds(tile * 8, 8), :], inner, axis=1, mode="promise_in_bounds"
+            source[pl.ds((first + tile) * 8, 8), :], inner, axis=1, mode="promise_in_bounds"
         )
         value = jnp.where(outer == tile, picked, value)
     return value
@@ -239,14 +239,9 @@
         return three, five
 
     def store_pair(target, index, first, three, five):
-        rows = slice(first, first + 16)
-        more = slice(width + first, width + first + 16)
-        high, low = split_two(five)
-        target[index, rows, 0:width] = high
-        target[index, rows, width : 2 * width] = low
-        high, low = split_two(three)
-        target[index, more, 0:width] = high
-        target[index, more, width : 2 * width] = low
+        for at, value in ((first, five), (width + first, three)):
+            for half, part in enumerate(split_two(value)):
+                target[index, at : at + 16, half * width : (half + 1) * width] = part
 
     def put_coefs(index, shift):
         def row(at):
@@ -325,11 +320,11 @@
             for first in range(0, width, 16):
                 three, five = pair_rows(found, first, False)
                 store_pair(pair_back, slot, first, three, five)
-            for part in (slice(0, width), slice(width, 2 * width)):
-                for half in (slice(0, width), slice(width, 2 * width)):
-                    pair_left[slot, part, half] = pair_back[slot, part, half].T
-
-    grouped(4, far_pairs)
+            for half in range(2):
+                for part in (slice(0, width), slice(width, 2 * width)):
+                    lanes = slice(half * width, (half + 1) * width)
+                    pair_left[slot, part, lanes] = pair_back[slot, part, lanes].T
+
 
     named_row = jnp.concatenate(
         [names_ref[entry + 1 : entry + 2, :] for entry in range(near)] * 3, axis=1
@@ -365,12 +360,18 @@
         )
         minus = jnp.concatenate([jnp.where(low_rows, 0.0, vec), jnp.zeros((8, width), F32)], axis=0)
         for part, value in enumerate(split_three(moments)):
-            blocks[tile, part * 16 : part * 16 + 16, 0:width] = value
+            blocks[tile, 0, part * 16 : part * 16 + 16, :] = value
         for part, value in enumerate(split_three(minus)):
-            blocks[tile, part * 16 : part * 16 + 16, width : 2 * width] = value
-
-    def product(tile, weights, index):
-        out = jnp.dot(blocks[tile], weights, preferred_element_type=F32)
+            blocks[tile, 1, part * 16 : part * 16 + 16, :] = value
+
+    def product(tile, pairs, slot, index):
+        block = blocks[tile]
+        weights = pairs[slot]
+        out = jnp.dot(
+            jnp.concatenate([block[0], block[1]], axis=1),
+            weights,
+            preferred_element_type=F32,
+        )
         out = out[:, :width] + out[:, width:]
         out = (out[0:16] + out[16:32]) + out[32:48]
         total = coefs[index, 0] * out[0:8] + coefs[index, 1] * out[8:16]
@@ -391,22 +392,36 @@
         make_block(tile)
         for entry in range(near):
             slot = entry * tiles + tile
-            fields[eight(slot), :] = product(tile, pair_back[slot], tiles + slot)
+            fields[eight(slot), :] = product(tile, pair_back, slot, tiles + slot)
 
     def own_step(tile):
-        summed[eight(tile), :] = product(tile, pair_own[tile], tile)
+        summed[eight(tile), :] = product(tile, pair_own, tile, tile)
 
     def left_step(tile):
         total = summed[eight(tile), :]
         for entry in range(near):
             slot = entry * tiles + tile
             named = list_ref[entry + 1, tile]
-            total = total + product(named, pair_left[slot], tiles + slots + slot)
+            total = total + product(named, pair_left, slot, tiles + slots + slot)
         summed[eight(tile), :] = total
 
+    put_vector(0, resid)
+
+    def far_group(group, carry):
+        for offset in range(4):
+            back_step(lax.rem(group * 4 + offset + tiles - 4, tiles))
+        for offset in range(4):
+            far_pairs(group * 4 + offset)
+        return carry
+
+    lax.fori_loop(0, tiles // 4, far_group, 0)
+    for offset in range(4):
+        back_step(tiles - 4 + offset)
+
     def applied(turn, vec):
-        put_vector(0, vec)
-        grouped(16, back_step)
+        if turn > 0:
+            put_vector(0, vec)
+            grouped(32, back_step)
         back = jnp.concatenate(
             [fields[pl.ds(axis, slots, stride=8), :] for axis in range(3)], axis=1
         )
@@ -422,7 +437,7 @@
         put_vector(tiles, ahead)
         for tile in range(tiles):
             make_block(tiles + tile)
-        grouped(16, left_step)
+        grouped(32, left_step)
         field = [
             summed[strided(0, axis), :] + spread[:tiles, axis * width : (axis + 1) * width]
             for axis in range(3)
@@ -430,13 +445,18 @@
         copy_f(turn).wait_recv()
         return [vec[axis] * alpha_inv - (field[axis] + back_f[turn, axis]) for axis in range(3)]
 
+    first_half = lax.broadcasted_iota(jnp.int32, (1, width), 1) < width // 2
+
     def dot_rows(left, right):
         total = left[0] * right[0] + left[1] * right[1] + left[2] * right[2]
         return jnp.sum(total, axis=0, keepdims=True)
 
     def send_dots(turn, resid, w):
+        norm_row, product_row = dot_rows(resid, resid), dot_rows(resid, w)
         dots[turn, 0] = jnp.where(
-            sub_ids == 0, dot_rows(resid, resid), jnp.where(sub_ids == 1, dot_rows(resid, w), 0.0)
+            first_half,
+            norm_row + pltpu.roll(norm_row, width // 2, 1),
+            product_row + pltpu.roll(product_row, width // 2, 1),
         )
 
         def send(step, carry):
@@ -455,6 +475,24 @@
     def wait_dots(turn, which):
         whole = dots.at[turn, pl.ds(1, count - 1)]
         pltpu.make_async_copy(whole, whole, dot_sem.at[which, turn]).wait()
+
+    def gather_last(solution, resid, direction, w, s):
+        for axis in range(3):
+            feat[strided(0, axis), :] = solution[axis]
+            feat[strided(0, 3 + axis), :] = resid[axis]
+            feat[strided(tiles, axis), :] = direction[axis]
+            feat[strided(tiles, 3 + axis), :] = s[axis]
+        for row, part in ((6, w[0]), (7, w[1]), (8 * tiles + 6, w[2])):
+            feat[pl.ds(row, tiles, stride=8), :] = part
+
+        feat[strided(tiles, 7), :] = w[2]
+
+        def fetch(tile):
+            row = inverse[pl.ds(tile, 1), :]
+            final[eight(tile), :] = gather_tile(row, feat, tiles)
+            final[eight(tiles + tile), :] = gather_tile(row, feat, tiles, tiles)
+
+        grouped(4, fetch)
 
     w = applied(0, resid)
     solution = direction = s = z = None
@@ -468,10 +506,12 @@
         send_dots(turn, resid, w)
         if more_turns:
             q = applied(turn + 1, w)
+        else:
+            gather_last(solution, resid, direction, w, s)
         wait_dots(turn, 1)
-        sums = jnp.sum(jnp.sum(dots[turn], axis=0), axis=1, keepdims=True)
-        norm = sums[0:1, :]
-        product_now = sums[1:2, :]
+        sums = jnp.sum(dots[turn], axis=0)
+        norm = jnp.sum(jnp.where(first_half, sums, 0.0), axis=1, keepdims=True)
+        product_now = jnp.sum(jnp.where(first_half, 0.0, sums), axis=1, keepdims=True)
         if turn == 0:
             step = norm / product_now
             direction, s = resid, w
@@ -481,6 +521,8 @@
         else:
             ratio = norm / norm_last
             step = norm / (product_now - ratio * norm / step_last)
+            if not more_turns:
+                break
             direction = [resid[axis] + ratio * direction[axis] for axis in range(3)]
             s = [w[axis] + ratio * s[axis] for axis in range(3)]
             solution = [solution[axis] + step * direction[axis] for axis in range(3)]
@@ -491,12 +533,14 @@
             w = [w[axis] - step * z[axis] for axis in range(3)]
         norm_last, step_last = norm, step
 
-    for axis in range(3):
-        final[strided(0, axis), :] = solution[axis]
-        final[strided(0, 3 + axis), :] = resid[axis]
+    plus = jnp.where(sub_ids < 3, 1.0, -1.0)
+    by_ratio = plus * (step * ratio)
+    by_step = plus * step
 
     def give(tile):
-        value = gather_tile(inverse[pl.ds(tile, 1), :], final, tiles)
+        first, second = final[eight(tile), :], final[eight(tiles + tile), :]
+        third = jnp.where(sub_ids == 5, pltpu.roll(second, 7, 0), pltpu.roll(first, 5, 0))
+        value = first + by_step * third + by_ratio * second
         lanes = pl.ds(pl.multiple_of(tile * width, width), width)
         dip_ref[:, lanes] = value[0:3]
         res_ref[:, lanes] = value[3:6]
@@ -530,9 +574,9 @@
         in_specs=[smem, smem, vmem, vmem, vmem, vmem, vmem],
         out_specs=(vmem, vmem),
         scratch_shapes=[
-            per_slab,
+            per_window,
             pltpu.VMEM((tiles, width), jnp.int32),
-            per_slab,
+            per_window,
             pltpu.VMEM((2 * tiles, width), F32),
             per_window,
             per_window,
@@ -546,7 +590,7 @@
             per_window,
             pltpu.VMEM(((1 + 2 * near) * tiles, 3, 8, width), F32),
             per_window,
-            pltpu.VMEM((2 * tiles, 48, 2 * width), BF16),
+            pltpu.VMEM((2 * tiles, 2, 48, width), BF16),
             pltpu.VMEM((near * tiles * 8, width), F32),
             per_slab,
             pltpu.VMEM((4, tiles, width), F32),
@@ -555,7 +599,7 @@
             vectors,
             vectors,
             vectors,
-            pltpu.VMEM((ITERS, count, 8, width), F32),
+            pltpu.VMEM((ITERS, count, 1, width), F32),
             pltpu.SemaphoreType.DMA((2,)),
             pltpu.SemaphoreType.DMA((2, ITERS)),
             pltpu.SemaphoreType.DMA((2, ITERS)),

time: 51.9 us -> 49.7 us (0.958)
  Pallas kernels: 48.9 us -> 46.7 us
    pallas_call x1, Pallas kernels: 48.9 us -> 46.7 us  [on_device(): pl.pallas_call(functools.partial(kernel, count, tiles, links), out_shape=...]
where the time goes in v4:
time: 49.7 us; the launch traced here: 49.5 us
  Pallas kernels  46.7 us (94%)
  local copies, waits for them, and re-layouts  2.15 us (4%)
  between operations  0.65 us (1%)
    pallas_call x1, Pallas kernels, on_device(): pl.pallas_call(functools.partial(kernel, count, tiles, links), out_shape=...  46.7 us
    unnamed x4, local copies, waits for them, and re-layouts  2.15 us

profile of v4, /device:TPU:0, one launch (start us, length us, event | category | flops | bytes accessed | tf_op | source)
XLA Modules:
  0.0 49.5 jit_solution(9603100559202233581)
XLA Ops:
  0.6 46.7 %shard_map.77 = (f32[3,4096]{1,0:T(4,128)}, f32[3,4096]{1,0:T(4,128)}) custom-call(s32[3,32]{1,0:T(4,128)} %bitcast.6, s32[3,2,32]{2,1,0:T(2,128)} %bitcast.8, s32[3,32]{1,0:T(4,128)} %bitcast.7, f32[3,4096]{1,0:T(4,128)} %place_ref.1, f32[1,4096]{1,0:T(1,128)} %bitcast.4, f32[3,4096]{1,0:T(4,128)} %field_ref.1, s32[32,128]{1,0:T(8,128)} %bitcast.5), custom_call_target="tpu_custom_call" | custom-call | tf_op jit(solution)/shard_map/pallas_call | solution.py:571
  47.3 0.0 copy-start
  47.3 1.5 %copy.10 = f32[3,4096]{1,0:T(4,128)} copy(f32[3,4096]{1,0:T(4,128)} %get-tuple-element.4) | data formatting | bytes 98304
  48.8 0.0 copy-done
  48.9 0.6 %copy.11 = f32[3,4096]{1,0:T(4,128)} copy(f32[3,4096]{1,0:T(4,128)S(1)} %copy-done) | data formatting | bytes 98304
Async XLA Ops:
  47.3 1.5 %copy-start = (f32[3,4096]{1,0:T(4,128)S(1)}, f32[3,4096]{1,0:T(4,128)}, u32[]{:S(2)}) copy-start(f32[3,4096]{1,0:T(4,128)} %get-tuple-element.5) | copy-start | bytes 147460

commit v5 on v4

--- a/solution.py
+++ b/solution.py
@@ -8,6 +8,7 @@
 from jax.sharding import PartitionSpec as P
 
 ITERS = 4
+FAR = 4
 MESH = pl.DeviceIdType.MESH
 thole_factor = 0.39
 LN2 = 0.6931471805599453
@@ -56,8 +57,7 @@
     polar_ref,
     field_ref,
     atom_ref,
-    dip_ref,
-    res_ref,
+    out_ref,
     feat,
     inverse,
     final,
@@ -408,17 +408,17 @@
     put_vector(0, resid)
 
     def far_group(group, carry):
-        for offset in range(4):
-            back_step(lax.rem(group * 4 + offset + tiles - 4, tiles))
-        for offset in range(4):
-            far_pairs(group * 4 + offset)
+        for offset in range(FAR):
+            back_step(lax.rem(group * FAR + offset + tiles - FAR, tiles))
+        for offset in range(FAR):
+            far_pairs(group * FAR + offset)
         return carry
 
-    lax.fori_loop(0, tiles // 4, far_group, 0)
-    for offset in range(4):
-        back_step(tiles - 4 + offset)
-
-    def applied(turn, vec):
+    lax.fori_loop(0, tiles // FAR, far_group, 0)
+    for offset in range(FAR):
+        back_step(tiles - FAR + offset)
+
+    def applied(turn, vec, meanwhile=None):
         if turn > 0:
             put_vector(0, vec)
             grouped(32, back_step)
@@ -431,6 +431,8 @@
         for axis in range(3):
             sent_f[turn, axis] = spread[tiles:, axis * width : (axis + 1) * width]
         copy_f(turn).start()
+        if meanwhile is not None:
+            meanwhile()
         grouped(32, own_step)
         copy_w(turn).wait_recv()
         ahead = [ahead_w[turn, axis] for axis in range(3)]
@@ -442,8 +444,7 @@
             summed[strided(0, axis), :] + spread[:tiles, axis * width : (axis + 1) * width]
             for axis in range(3)
         ]
-        copy_f(turn).wait_recv()
-        return [vec[axis] * alpha_inv - (field[axis] + back_f[turn, axis]) for axis in range(3)]
+        return [vec[axis] * alpha_inv - field[axis] for axis in range(3)]
 
     first_half = lax.broadcasted_iota(jnp.int32, (1, width), 1) < width // 2
 
@@ -495,6 +496,8 @@
         grouped(4, fetch)
 
     w = applied(0, resid)
+    copy_f(0).wait_recv()
+    w = [w[axis] - back_f[0, axis] for axis in range(3)]
     solution = direction = s = z = None
     norm_last = step_last = None
     for turn in range(ITERS):
@@ -503,10 +506,10 @@
             for axis in range(3):
                 sent_w[turn + 1, axis] = w[axis]
             copy_w(turn + 1).start()
-        send_dots(turn, resid, w)
-        if more_turns:
+            send_dots(turn, resid, w)
             q = applied(turn + 1, w)
         else:
+            send_dots(turn, resid, w)
             gather_last(solution, resid, direction, w, s)
         wait_dots(turn, 1)
         sums = jnp.sum(dots[turn], axis=0)
@@ -526,11 +529,14 @@
             direction = [resid[axis] + ratio * direction[axis] for axis in range(3)]
             s = [w[axis] + ratio * s[axis] for axis in range(3)]
             solution = [solution[axis] + step * direction[axis] for axis in range(3)]
-            if more_turns:
-                z = [q[axis] + ratio * z[axis] for axis in range(3)]
+            z = [q[axis] + ratio * z[axis] for axis in range(3)]
         resid = [resid[axis] - step * s[axis] for axis in range(3)]
         if more_turns:
             w = [w[axis] - step * z[axis] for axis in range(3)]
+            copy_f(turn + 1).wait_recv()
+            late = [back_f[turn + 1, axis] for axis in range(3)]
+            w = [w[axis] + step * late[axis] for axis in range(3)]
+            z = [z[axis] - late[axis] for axis in range(3)]
         norm_last, step_last = norm, step
 
     plus = jnp.where(sub_ids < 3, 1.0, -1.0)
@@ -542,8 +548,7 @@
         third = jnp.where(sub_ids == 5, pltpu.roll(second, 7, 0), pltpu.roll(first, 5, 0))
         value = first + by_step * third + by_ratio * second
         lanes = pl.ds(pl.multiple_of(tile * width, width), width)
-        dip_ref[:, lanes] = value[0:3]
-        res_ref[:, lanes] = value[3:6]
+        out_ref[:, lanes] = value[0:6]
 
     grouped(8, give)
 
@@ -563,16 +568,16 @@
     pairs = (2 * width, 2 * width)
     vmem = pl.BlockSpec(memory_space=pltpu.VMEM)
     smem = pl.BlockSpec(memory_space=pltpu.SMEM)
-    out = jax.ShapeDtypeStruct((3, atoms), F32)
+    out = jax.ShapeDtypeStruct((6, atoms), F32)
     vectors = pltpu.VMEM((ITERS, 3, tiles, width), F32)
     per_slab = pltpu.VMEM((tiles * 8, width), F32)
     per_window = pltpu.VMEM((2 * tiles * 8, width), F32)
     names = tile_list.T
-    return pl.pallas_call(
+    both = pl.pallas_call(
         functools.partial(kernel, count, tiles, links),
-        out_shape=(out, out),
+        out_shape=out,
         in_specs=[smem, smem, vmem, vmem, vmem, vmem, vmem],
-        out_specs=(vmem, vmem),
+        out_specs=vmem,
         scratch_shapes=[
             per_window,
             pltpu.VMEM((tiles, width), jnp.int32),
@@ -615,6 +620,7 @@
         field_ext,
         tile_atom.reshape(tiles, width),
     )
+    return both[:3], both[3:]
 
 
 def solution(mesh):

time: 49.7 us -> 49 us (0.986)
    unnamed x4 -> x0, local copies, waits for them, and re-layouts: 2.15 us -> none
    slice x0 -> x1, local copies, waits for them, and re-layouts: none -> 1.66 us  [on_device(): return (both[:3], both[3:])]
where the time goes in v5:
time: 49 us; the launch traced here: 48.8 us
  Pallas kernels  46.5 us (95%)
  local copies, waits for them, and re-layouts  1.66 us (3%)
  between operations  0.64 us (1%)
    pallas_call x1, Pallas kernels, on_device(): pl.pallas_call(functools.partial(kernel, count, tiles, links), out_shape=...  46.5 us
    slice x1, local copies, waits for them, and re-layouts, on_device(): return (both[:3], both[3:])  1.66 us

profile of v5, /device:TPU:0, one launch (start us, length us, event | category | flops | bytes accessed | tf_op | source)
XLA Modules:
  0.0 48.8 jit_solution(837691200637740198)
XLA Ops:
  0.6 46.5 %shard_map.77 = f32[6,4096]{1,0:T(8,128)} custom-call(s32[3,32]{1,0:T(4,128)} %bitcast.6, s32[3,2,32]{2,1,0:T(2,128)} %bitcast.8, s32[3,32]{1,0:T(4,128)} %bitcast.7, f32[3,4096]{1,0:T(4,128)} %place_ref.1, f32[1,4096]{1,0:T(1,128)} %bitcast.4, f32[3,4096]{1,0:T(4,128)} %field_ref.1, s32[32,128]{1,0:T(8,128)} %bitcast.5), custom_call_target="tpu_custom_call" | custom-call | tf_op jit(solution)/shard_map/pallas_call | solution.py:576
  47.2 1.7 %fusion = (f32[3,4096]{1,0:T(4,128)}, f32[3,4096]{1,0:T(4,128)}) fusion(f32[6,4096]{1,0:T(8,128)} %shard_map.77), kind=kLoop, calls=%fused_computation | loop fusion | bytes 196608 | tf_op jit(solution)/shard_map/slice | solution.py:623

commit v6 on v5

--- a/solution.py
+++ b/solution.py
@@ -50,6 +50,13 @@
     count,
     tiles,
     links,
+    list_hbm,
+    shift_hbm,
+    place_hbm,
+    polar_hbm,
+    field_hbm,
+    atom_hbm,
+    out_any,
     list_ref,
     shift_ref,
     names_ref,
@@ -58,6 +65,8 @@
     field_ref,
     atom_ref,
     out_ref,
+    in_sem,
+    out_sem,
     feat,
     inverse,
     final,
@@ -96,6 +105,23 @@
     after = lax.rem(me + 1, count)
     before = lax.rem(me + count - 1, count)
 
+    arrivals = [
+        pltpu.make_async_copy(source, target, in_sem.at[at])
+        for at, (source, target) in enumerate(
+            (
+                (place_hbm, place_ref),
+                (field_hbm, field_ref),
+                (polar_hbm, polar_ref),
+                (atom_hbm, atom_ref),
+                (list_hbm, list_ref),
+                (shift_hbm, shift_ref),
+                (list_hbm, names_ref),
+            )
+        )
+    ]
+    for arrival in arrivals:
+        arrival.start()
+
     barrier = pltpu.get_barrier_semaphore()
 
     def greet(step, carry):
@@ -120,6 +146,8 @@
 
         lax.fori_loop(0, tiles // size, step, 0)
 
+    for arrival in arrivals[:4]:
+        arrival.wait()
     for tile in range(tiles):
         lanes = pl.ds(tile * width, width)
         feat[tile * 8 : tile * 8 + 3, :] = place_ref[:, lanes]
@@ -289,6 +317,8 @@
     lax.fori_loop(0, tiles // 8, invert_step, 0)
     inverse[...] = (found_ref[:tiles] * float(width) + found_ref[tiles:]).astype(jnp.int32)
 
+    for arrival in arrivals[4:]:
+        arrival.wait()
     copy_p().wait_recv()
     for at, row in enumerate(pair_inputs):
         window[strided(tiles, row), :] = ahead_p[at]
@@ -557,6 +587,9 @@
         copy_w(turn).wait_send()
         copy_f(turn).wait_send()
         wait_dots(turn, 0)
+    leave = pltpu.make_async_copy(out_ref, out_any, out_sem)
+    leave.start()
+    leave.wait()
 
 
 def on_device(positions, polar, field_ext, tile_atom, tile_list, image_shift):
@@ -566,8 +599,6 @@
     near = links - 1
     count = lax.axis_size("gx")
     pairs = (2 * width, 2 * width)
-    vmem = pl.BlockSpec(memory_space=pltpu.VMEM)
-    smem = pl.BlockSpec(memory_space=pltpu.SMEM)
     out = jax.ShapeDtypeStruct((6, atoms), F32)
     vectors = pltpu.VMEM((ITERS, 3, tiles, width), F32)
     per_slab = pltpu.VMEM((tiles * 8, width), F32)
@@ -576,9 +607,19 @@
     both = pl.pallas_call(
         functools.partial(kernel, count, tiles, links),
         out_shape=out,
-        in_specs=[smem, smem, vmem, vmem, vmem, vmem, vmem],
-        out_specs=vmem,
+        in_specs=[pl.BlockSpec(memory_space=pltpu.HBM)] * 6,
+        out_specs=pl.BlockSpec(memory_space=pl.ANY),
         scratch_shapes=[
+            pltpu.SMEM((links, tiles), jnp.int32),
+            pltpu.SMEM((links, 2, tiles), jnp.int32),
+            pltpu.VMEM((links, tiles), jnp.int32),
+            pltpu.VMEM((3, atoms), F32),
+            pltpu.VMEM((1, atoms), F32),
+            pltpu.VMEM((3, atoms), F32),
+            pltpu.VMEM((tiles, width), jnp.int32),
+            pltpu.VMEM((6, atoms), F32),
+            pltpu.SemaphoreType.DMA((7,)),
+            pltpu.SemaphoreType.DMA,
             per_window,
             pltpu.VMEM((tiles, width), jnp.int32),
             per_window,
@@ -610,11 +651,12 @@
             pltpu.SemaphoreType.DMA((2, ITERS)),
             pltpu.SemaphoreType.DMA((2, ITERS)),
         ],
-        compiler_params=pltpu.CompilerParams(collective_id=0, has_side_effects=True),
+        compiler_params=pltpu.CompilerParams(
+            collective_id=0, has_side_effects=True
+        ),
     )(
         names,
         image_shift.transpose(2, 0, 1),
-        names,
         positions,
         polar.reshape(1, atoms),
         field_ext,

time: 49 us -> 48.3 us (0.986)
  Pallas kernels: 46.5 us -> 45.8 us
    pallas_call x1, Pallas kernels: 46.5 us -> 45.8 us  [on_device(): pl.pallas_call(functools.partial(kernel, count, tiles, links), out_shape=...]
where the time goes in v6:
time: 48.3 us; the launch traced here: 48.1 us
  Pallas kernels  45.8 us (95%)
  local copies, waits for them, and re-layouts  1.66 us (3%)
  between operations  0.64 us (1%)
    pallas_call x1, Pallas kernels, on_device(): pl.pallas_call(functools.partial(kernel, count, tiles, links), out_shape=...  45.8 us
    slice x1, local copies, waits for them, and re-layouts, on_device(): return (both[:3], both[3:])  1.66 us

profile of v6, /device:TPU:0, one launch (start us, length us, event | category | flops | bytes accessed | tf_op | source)
XLA Modules:
  0.0 48.1 jit_solution(12166992733081342219)
XLA Ops:
  0.6 45.8 %shard_map.77 = f32[6,4096]{1,0:T(8,128)} custom-call(s32[3,32]{1,0:T(4,128)} %bitcast.7, s32[3,2,32]{2,1,0:T(2,128)} %bitcast.6, f32[3,4096]{1,0:T(4,128)} %place_hbm.1, f32[1,4096]{1,0:T(1,128)} %bitcast.4, f32[3,4096]{1,0:T(4,128)} %field_hbm.1, s32[32,128]{1,0:T(8,128)} %bitcast.5), custom_call_target="tpu_custom_call" | custom-call | tf_op jit(solution)/shard_map/pallas_call | solution.py:607
  46.5 1.7 %fusion = (f32[3,4096]{1,0:T(4,128)}, f32[3,4096]{1,0:T(4,128)}) fusion(f32[6,4096]{1,0:T(8,128)} %shard_map.77), kind=kLoop, calls=%fused_computation | loop fusion | bytes 196608 | tf_op jit(solution)/shard_map/slice | solution.py:665
